TPU v7x, 256 devices: a 8x8x2 block of a 8x8x16 slice. The times are simulated.
256 devices in a mesh: parts: 2 (over z), seq: 128 (over x, y, core).
Axes of the slice: x: 8, y: 8, z: 2, core: 2. Of those that a mesh axis runs over, the one named last changes fastest.
The devices are a block of a 8x8x16 slice.
Arguments:
- token_ids: int32 [4, 4], P(None, 'parts'), parts along dimension 1, may hold values from 0 to 76031
- lengths: int32 [4], P('parts'), parts along dimension 0, may hold values from 24576 to 32768, as said below
- embed_table: bfloat16 [76032, 5120], P('seq'), may hold values from -6 to 6
- attn_gain: bfloat16 [5120], replicated, may hold values from 0.25 to 1.75
- w_qkv: bfloat16 [5120, 7168], P('seq'), may hold values from -0.3125 to 0.3125
- qkv_bias: float32 [7168], replicated, may hold values from -8 to 8
- cache_keys: bfloat16 [4, 32768, 1024], P('parts', 'seq'), parts along dimension 0, may hold values from -300 to 300
- cache_values: bfloat16 [4, 32768, 1024], P('parts', 'seq'), parts along dimension 0, may hold values from -6 to 6
- w_out: bfloat16 [5120, 5120], P(None, 'seq'), may hold values from -0.078125 to 0.078125
- mlp_gain: bfloat16 [5120], replicated, may hold values from 0.25 to 1.75
- w_gate: bfloat16 [5120, 16384], P(None, 'seq'), may hold values from -0.078125 to 0.078125
- w_up: bfloat16 [5120, 16384], P(None, 'seq'), may hold values from -0.078125 to 0.078125
- w_down: bfloat16 [16384, 5120], P('seq'), may hold values from -0.1875 to 0.1875
Outputs:
- attended: bfloat16 [4, 4, 5120], P(None, 'parts'), parts along dimension 1
- layer_out: bfloat16 [4, 4, 5120], P(None, 'parts', 'seq'), parts along dimension 1
There are 2 independent parts, one for each index of `parts`. A program takes and returns all parts, laid end to end along the dimension named above; an argument that names none is the same for every part. Nothing has to cross between parts.
Inputs may be any that keep to these rules, and one draw needn't show every extreme that they name: Cache positions lengths[b] and later are unused; the first prompt fills the whole cache of 32768 positions.
All inputs are finite; a program needn't handle non-finite values.
Results may differ from a plain program's by a relative error of at most 0.017.
The roundings to bfloat16 on the way count: a program that leaves them out, or rounds other values in their place, can miss the bound.
Values may be sent and summed in bfloat16 or wider, within the bound.
A program may use at most 128 MiB of HBM per device.

v0:
```python
import math

import jax
import jax.numpy as jnp
from jax import lax
from jax.sharding import Mesh
from jax.sharding import PartitionSpec as P

HEADS = 40
KV_HEADS = 8
HEAD_DIM = 128
SEQ = ("seq_0", "seq_1", "seq_2")


NORM_EPS = 1e-06
ROPE_BASE = 1000000.0
MASKED = -1e30


def gathered_once(array, axis):
    leaves = jax.tree.leaves(array)
    order = sorted(range(len(leaves)), key=lambda k: -leaves[k].size)
    width = (1, *leaves[order[0]].shape)[-1]
    lines = [
        jnp.pad(leaves[k].reshape(-1), (0, -leaves[k].size % width)).reshape(-1, width)
        for k in order
    ]
    both, at, found = (lax.all_gather(jnp.concatenate(lines), axis), 0, {})
    for k, line in zip(order, lines):
        slab = both[:, at : at + len(line)].reshape(len(both), -1)
        found[k] = slab[:, : leaves[k].size].reshape(-1, *leaves[k].shape)
        at += len(line)
    numbers = iter(range(len(leaves)))
    return jax.tree.map(lambda _: found[next(numbers)], array)


def combined_by_axis(array, axes, combine):
    for axis in axes:
        pieces = gathered_once(array, axis)
        array = jax.tree.map(lambda part: part[0], pieces)
        for k in range(1, lax.axis_size(axis)):
            array = combine(array, jax.tree.map(lambda part: part[k], pieces))
    return array


def sum_in_order(parts, axes, order):
    dims = [lax.axis_size(a) for a in axes]
    parts = parts.reshape(*dims, *parts.shape[1:])
    parts = parts.transpose(*order, *range(len(axes), parts.ndim))
    parts = parts.reshape(-1, *parts.shape[len(axes) :])
    for k in order:
        parts = lax.psum_scatter(parts, axes[k], scatter_dimension=0, tiled=True)
    return parts[0]


def cut_along(array, dim, devices):
    before, after = (array.shape[:dim], array.shape[dim + 1 :])
    return jnp.moveaxis(array.reshape(*before, devices, -1, *after), dim, 0)


def scatter_axes(array, axes, order, dim):
    devices = lax.axis_size(axes)
    return sum_in_order(cut_along(array, dim, devices), axes, order)


def rms_normalize(rows, gain):
    mean_square = jnp.mean(rows * rows, axis=-1, keepdims=True)
    return (rows * lax.rsqrt(mean_square + NORM_EPS) * gain.astype(jnp.float32)).astype(
        jnp.bfloat16
    )


def rotate(vectors, positions):
    half_dim = vectors.shape[-1] // 2
    frequency = ROPE_BASE ** (-2.0 * jnp.arange(half_dim, dtype=jnp.float32) / vectors.shape[-1])
    angles = positions.astype(jnp.float32)[..., None, None] * frequency
    cosine = jnp.cos(angles)
    sine_part = jnp.sin(angles)
    widened = vectors.astype(jnp.float32)
    first_half = widened[..., :half_dim]
    second = widened[..., half_dim:]
    joined = jnp.concatenate(
        [first_half * cosine - second * sine_part, second * cosine + first_half * sine_part],
        axis=-1,
    )
    return joined.astype(jnp.bfloat16)


def combine_partials(earlier, latter):
    top_one, total_one, sum_one = earlier
    top_two, total_two, sum_two = latter
    joined_top = jnp.maximum(top_one, top_two)
    scale_one = jnp.exp(top_one - joined_top)
    scale_two = jnp.exp(top_two - joined_top)
    return (
        joined_top,
        total_one * scale_one + total_two * scale_two,
        sum_one * scale_one[..., None] + sum_two * scale_two[..., None],
    )


def body(
    token_ids,
    lengths,
    embed_table,
    attn_gain,
    w_qkv,
    qkv_bias,
    cache_keys,
    cache_values,
    w_out,
    mlp_gain,
    w_gate,
    w_up,
    w_down,
):
    rank = lax.axis_index(SEQ)
    step_count, batch_count = token_ids.shape
    model_width = embed_table.shape[1]
    vocab_rows = embed_table.shape[0]
    query_width = HEADS * HEAD_DIM
    key_width = KV_HEADS * HEAD_DIM
    group_size = HEADS // KV_HEADS
    local_ids = token_ids - rank * vocab_rows
    inside = (local_ids >= 0) & (local_ids < vocab_rows)
    picked = jnp.take(embed_table, jnp.clip(local_ids, 0, vocab_rows - 1), axis=0)
    partial_rows = jnp.where(inside[..., None], picked.astype(jnp.float32), 0.0)
    stream = lax.psum(partial_rows, SEQ)
    normed = rms_normalize(stream, attn_gain).reshape(-1, model_width)
    feature_rows = w_qkv.shape[0]
    normed_local = lax.dynamic_slice_in_dim(normed, rank * feature_rows, feature_rows, 1)
    joint_partial = jnp.dot(normed_local, w_qkv, preferred_element_type=jnp.float32)
    joint_summed = lax.psum(joint_partial, SEQ)
    joint = (joint_summed + qkv_bias).astype(jnp.bfloat16).reshape(step_count, batch_count, -1)
    query_part = joint[..., :query_width].reshape(step_count, batch_count, HEADS, HEAD_DIM)
    key_part = joint[..., query_width : query_width + key_width].reshape(
        step_count, batch_count, KV_HEADS, HEAD_DIM
    )
    value_part = joint[..., query_width + key_width :].reshape(
        step_count, batch_count, KV_HEADS, HEAD_DIM
    )
    positions = lengths[None, :] + jnp.arange(step_count, dtype=jnp.int32)[:, None]
    queries = rotate(query_part, positions)
    new_keys = rotate(key_part, positions)
    grouped = queries.reshape(step_count, batch_count, KV_HEADS, group_size, HEAD_DIM)
    score_scale = 1.0 / math.sqrt(HEAD_DIM)
    local_len = cache_keys.shape[1]
    key_blocks = cache_keys.reshape(batch_count, local_len, KV_HEADS, HEAD_DIM)
    value_blocks = cache_values.reshape(batch_count, local_len, KV_HEADS, HEAD_DIM)
    scores = (
        jnp.einsum("sbkgd,bpkd->bkgsp", grouped, key_blocks, preferred_element_type=jnp.float32)
        * score_scale
    )
    places = rank * local_len + jnp.arange(local_len, dtype=jnp.int32)
    valid = (places[None, :] < lengths[:, None])[:, None, None, None, :]
    masked = jnp.where(valid, scores, MASKED)
    local_top = jnp.max(masked, axis=-1)
    weights = jnp.where(valid, jnp.exp(masked - local_top[..., None]), 0.0)
    local_total = jnp.sum(weights, axis=-1)
    local_sum = jnp.einsum(
        "bkgsp,bpkd->bkgsd",
        weights.astype(jnp.bfloat16),
        value_blocks,
        preferred_element_type=jnp.float32,
    )
    merged_top, merged_total, merged_sum = combined_by_axis(
        (local_top, local_total, local_sum), SEQ, combine_partials
    )
    new_scores = (
        jnp.einsum("sbkgd,tbkd->bkgst", grouped, new_keys, preferred_element_type=jnp.float32)
        * score_scale
    )
    step_index = jnp.arange(step_count, dtype=jnp.int32)
    causal = step_index[:, None] >= step_index[None, :]
    new_masked = jnp.where(causal, new_scores, MASKED)
    final_top = jnp.maximum(merged_top, jnp.max(new_masked, axis=-1))
    rescale = jnp.exp(merged_top - final_top)
    new_weights = jnp.where(causal, jnp.exp(new_masked - final_top[..., None]), 0.0)
    final_total = merged_total * rescale + jnp.sum(new_weights, axis=-1)
    final_sum = merged_sum * rescale[..., None] + jnp.einsum(
        "bkgst,tbkd->bkgsd",
        new_weights.astype(jnp.bfloat16),
        value_part,
        preferred_element_type=jnp.float32,
    )
    attended = jnp.transpose(final_sum / final_total[..., None], (3, 0, 1, 2, 4))
    attended = attended.reshape(step_count, batch_count, query_width).astype(jnp.bfloat16)
    shard_cols = w_out.shape[1]
    projected = jnp.dot(
        attended.reshape(-1, query_width), w_out, preferred_element_type=jnp.float32
    )
    stream_shard = lax.dynamic_slice_in_dim(stream, rank * shard_cols, shard_cols, 2)
    mid_shard = stream_shard + projected.reshape(step_count, batch_count, shard_cols)
    mid_rows = lax.all_gather(mid_shard, SEQ, axis=2, tiled=True)
    normed_mid = rms_normalize(mid_rows, mlp_gain)
    flat_rows = normed_mid.reshape(-1, model_width)
    gate = jnp.dot(flat_rows, w_gate, preferred_element_type=jnp.float32)
    upper = jnp.dot(flat_rows, w_up, preferred_element_type=jnp.float32)
    hidden = (jax.nn.silu(gate) * upper).astype(jnp.bfloat16)
    down_terms = jnp.dot(hidden, w_down, preferred_element_type=jnp.float32).reshape(
        step_count, batch_count, model_width
    )
    summed = scatter_axes(down_terms, SEQ, (2, 1, 0), 2)
    layer_out = (mid_shard + summed).astype(jnp.bfloat16)
    return (attended, layer_out)


def solution(mesh):
    finer = Mesh(
        mesh.devices.reshape(mesh.shape["parts"], 8, 8, 2), ("parts", "seq_0", "seq_1", "seq_2")
    )
    return jax.shard_map(
        body,
        mesh=finer,
        in_specs=(
            P(None, "parts"),
            P("parts"),
            P(SEQ, None),
            P(),
            P(SEQ, None),
            P(),
            P("parts", SEQ, None),
            P("parts", SEQ, None),
            P(None, SEQ),
            P(),
            P(None, SEQ),
            P(None, SEQ),
            P(SEQ, None),
        ),
        out_specs=(P(None, "parts", None), P(None, "parts", SEQ)),
        check_vma=False,
    )
```

profile of v0, /device:TPU:513, one launch (start us, length us, event | category | flops | bytes accessed | tf_op | source)
XLA Modules:
  0.0 707.2 jit_solution(17745230185070453889)
XLA Ops:
  7.3 0.8 compare_and_fusion
  8.3 4.2 gather_fusion
  12.8 0.8 convert_select_fusion
  14.4 1.1 copy-done.3
  15.8 1.1 bitcast_bitcast_fusion
  16.9 199.0 %all-reduce.14.cloned.1.call-done = f32[4,2,5120]{2,1,0:T(2,128)} async-done(((f32[4,2,5120]{2,1,0:T(2,128)}), f32[4,2,5120]{2,1,0:T(2,128)}) %all-reduce.14.cloned.1.call-update) | async-done | bytes 163856 | tf_op jit(solution)/shard_map/psum | solution.py:128
  215.8 1.1 multiply_reduce_fusion.1
  216.9 1.1 multiply_convert_fusion.1
  218.1 1.0 fusion.77
  219.2 180.9 %all-reduce.16.cloned.1.call-done = f32[8,7168]{1,0:T(8,128)} async-done(((f32[8,7168]{1,0:T(8,128)}), f32[8,7168]{1,0:T(8,128)}) %all-reduce.16.cloned.1.call-update) | async-done | bytes 229392 | tf_op jit(solution)/shard_map/psum | solution.py:133
  400.2 1.0 add_convert_fusion
  403.0 1.5 fusion.9
  405.4 32.7 %all-gather.9.cloned.1.call-done = f32[8,326,128]{2,1,0:T(8,128)} async-done(((f32[1,326,128]{2,1,0:T(8,128)}), f32[8,326,128]{2,1,0:T(8,128)}) %all-gather.9.cloned.1.call-update) | async-done | bytes 1335312 | tf_op jit(solution)/shard_map/all_gather | solution.py:28
  438.1 0.8 fusion.88
  439.2 2.0 fusion.39
  441.2 0.7 maximum_bitcast_fusion.1
  442.2 0.8 fusion.93
  443.1 38.4 %all-gather.11.cloned.1.call-done = f32[8,326,128]{2,1,0:T(8,128)} async-done(((f32[1,326,128]{2,1,0:T(8,128)}), f32[8,326,128]{2,1,0:T(8,128)}) %all-gather.11.cloned.1.call-update) | async-done | bytes 1335312 | tf_op jit(solution)/shard_map/all_gather | solution.py:28
  481.5 0.8 fusion.87
  482.6 2.0 fusion.18
  484.6 7.5 %all-gather.5 = f32[2,326,128]{2,1,0:T(8,128)S(1)} all-gather(f32[1,326,128]{2,1,0:T(8,128)S(1)} %maximum_bitcast_fusion.2), channel_id=4, replica_groups=mesh['parts'=2,'seq_0'=8,'seq_1'=8,'seq_2'=2] {'seq_2'}, dimensions={0}, use_global_device_ids=true | all-gather | bytes 500736 | tf_op jit(solution)/shard_map/all_gather | solution.py:28
  495.2 1.0 convolution_add_fusion.1
  496.3 57.3 %all_gather.27 = f32[4,2,5120]{0,1,2:T(2,128)} all-gather(f32[4,2,40]{0,1,2:T(2,128)S(1)} %copy.230), channel_id=1, replica_groups=mesh['parts'=2,'seq_0'=8,'seq_1'=8,'seq_2'=2] {'seq_0','seq_1','seq_2'}, dimensions={2}, use_global_device_ids=true | all-gather | bytes 165120 | tf_op jit(solution)/shard_map/all_gather | solution.py:194
  553.6 5.6 copy.233
  559.3 7.0 multiply_reduce_fusion
  567.0 1.9 fusion.8
  569.5 1.1 copy.236
  572.1 30.6 %all-reduce.18.cloned.1.call-done = f32[128,4,2,40]{3,1,2,0:T(4,128)} async-done(((f32[128,4,2,40]{3,1,2,0:T(4,128)}), f32[128,4,2,40]{3,1,2,0:T(4,128)}) %all-reduce.18.cloned.1.call-update) | async-done | bytes 163856
  602.7 1.7 constant_dynamic-slice_fusion.2
  606.3 69.4 %all-reduce.20.cloned.1.call-done = f32[64,4,2,40]{3,1,2,0:T(4,128)} async-done(((f32[64,4,2,40]{3,1,2,0:T(4,128)}), f32[64,4,2,40]{3,1,2,0:T(4,128)}) %all-reduce.20.cloned.1.call-update) | async-done | bytes 81936
  675.7 0.8 constant_dynamic-slice_fusion.1
  676.5 22.6 %all-reduce.8 = f32[8,4,2,40]{3,1,2,0:T(4,128)S(1)} all-reduce(f32[8,4,2,40]{3,1,2,0:T(4,128)S(1)} %constant_dynamic-slice_fusion.1), channel_id=7, replica_groups=mesh['parts'=2,'seq_0'=8,'seq_1'=8,'seq_2'=2] {'seq_0'}, use_global_device_ids=true, to_apply=%region_10.11.clone | all-reduce | flops 2560 | bytes 20480
  (137 shorter events, 12.8 us)
Async XLA Ops:
  7.2 559.9 %copy-start = (bf16[128,5120]{1,0:T(8,128)(2,1)S(1)}, bf16[128,5120]{1,0:T(8,128)(2,1)}, u32[]{:S(2)}) copy-start(bf16[128,5120]{1,0:T(8,128)(2,1)} %param.25) | copy-start | bytes 3932164
  7.2 6.6 copy-start.7
  7.2 6.6 copy-start.9
  7.2 6.8 copy-start.2
  7.2 208.6 %all-reduce.14.cloned.1.call-start = ((), (), s32[]{:S(2)}) async-start(), calls=%async_computation | async-start | bytes 327680 | tf_op jit(solution)/shard_map/psum | solution.py:128
  13.7 386.5 %all-reduce.16.cloned.1.call-start = ((), (), s32[]{:S(2)}) async-start(), calls=%async_computation.1 | async-start | bytes 458752 | tf_op jit(solution)/shard_map/psum | solution.py:133
  14.3 1.2 copy-start.3
  15.8 202.2 %copy-start.4 = (bf16[40,7168]{1,0:T(8,128)(2,1)S(1)}, bf16[40,7168]{1,0:T(8,128)(2,1)}, u32[]{:S(2)}) copy-start(bf16[40,7168]{1,0:T(8,128)(2,1)} %param.17) | copy-start | bytes 1720324
  16.9 383.3 %copy-start.6 = (f32[7168]{0:T(1024)S(1)}, f32[7168]{0:T(1024)}, u32[]{:S(2)}) copy-start(f32[7168]{0:T(1024)} %param.18) | copy-start | bytes 86020
  219.1 219.0 %all-gather.9.cloned.1.call-start = ((), (), s32[]{:S(2)}) async-start(), calls=%async_computation.2 | async-start | bytes 1511424 | tf_op jit(solution)/shard_map/all_gather | solution.py:28
  405.2 36.8 %copy-start.8 = (bf16[5120]{0:T(1024)(128)(2,1)S(1)}, bf16[5120]{0:T(1024)(128)(2,1)}, u32[]{:S(2)}) copy-start(bf16[5120]{0:T(1024)(128)(2,1)} %param.22) | copy-start | bytes 30724
  405.3 76.2 %all-gather.11.cloned.1.call-start = ((), (), s32[]{:S(2)}) async-start(), calls=%async_computation.3 | async-start | bytes 1511424 | tf_op jit(solution)/shard_map/all_gather | solution.py:28
  441.9 160.7 %all-reduce.18.cloned.1.call-start = ((), (), s32[]{:S(2)}) async-start(), calls=%async_computation.4 | async-start | bytes 1048576
  494.2 1.0 copy-start.10
  495.2 58.4 %copy-start.5 = (bf16[4,2,5120]{2,1,0:T(2,128)(2,1)}, bf16[4,2,5120]{2,1,0:T(2,128)(2,1)S(1)}, u32[]{:S(2)}) copy-start(bf16[4,2,5120]{2,1,0:T(2,128)(2,1)S(1)} %convert_element_type.84) | copy-start | bytes 245764
  559.3 7.5 %copy-start.1 = (bf16[5120,128]{1,0:T(8,128)(2,1)S(1)}, bf16[5120,128]{1,0:T(8,128)(2,1)}, u32[]{:S(2)}) copy-start(bf16[5120,128]{1,0:T(8,128)(2,1)} %param.23) | copy-start | bytes 3932164
  569.3 1.5 copy-start.13
  569.5 34.9 %copy-start.12 = (u32[256]{0:T(256)S(1)}, u32[256]{0:T(256)}, u32[]{:S(2)}) copy-start(u32[256]{0:T(256)} %constant.90) | copy-start | bytes 3076
  569.5 35.5 %copy-start.11 = (u32[256]{0:T(256)S(1)}, u32[256]{0:T(256)}, u32[]{:S(2)}) copy-start(u32[256]{0:T(256)} %constant.94) | copy-start | bytes 3076
  570.7 105.0 %all-reduce.20.cloned.1.call-start = ((), (), s32[]{:S(2)}) async-start(), calls=%async_computation.5 | async-start | bytes 524288
Sparse Core Ops, SparseCore 0:
  13.8 202.0 all-reduce.13
  219.2 180.9 all-reduce.15
  405.4 32.6 all-gather.8
  442.0 39.4 all-gather.10
  570.9 31.7 all-reduce.17
  604.9 70.8 all-reduce.19
where the time goes:
time: 718 us; the launch traced here: 707 us
  waiting for transfers between devices  551 us (77%)
  blocking collectives  87.5 us (12%)
  local copies, waits for them, and re-layouts  25.4 us (4%)
  other arithmetic  19.2 us (3%)
  between operations  16 us (2%)
  matrix products  7.37 us (1%)
    psum x1, waiting for transfers between devices, body(): stream = lax.psum(partial_rows, SEQ)  199 us
    psum x1, waiting for transfers between devices, body(): joint_summed = lax.psum(joint_partial, SEQ)  181 us
    unnamed x8, waiting for transfers between devices  100 us
    all_gather x2, waiting for transfers between devices, gathered_once(): both, at, found = (lax.all_gather(jnp.concatenate(lines), axis), 0, {})  71.1 us
    all_gather x1, blocking collectives, body(): mid_rows = lax.all_gather(mid_shard, SEQ, axis=2, tiled=True)  57.3 us
    unnamed x1, blocking collectives  22.6 us
  transfers between devices with their start and end apart: 6, of which 6 were waited for; matrix products, arithmetic and copies ran while one was open for 1% of the time, Pallas kernels for 0%

commit v1 on v0

v1 whole, which is shorter than its diff:
```python
import functools
import math

import jax
import jax.numpy as jnp
import numpy as np
from jax import lax
from jax.experimental import pallas as pl
from jax.experimental.pallas import tpu as pltpu
from jax.sharding import PartitionSpec as P

HEADS = 40
KV_HEADS = 8
HEAD_DIM = 128
NORM_EPS = 1e-06
ROPE_BASE = 1000000.0
MASKED = -1e30

ROWS = 8
LANES = 128
XS, YS, CORES = 8, 8, 2
PLANE = YS * CORES
CHIPS = XS * YS
GROUP = CHIPS * CORES
JOINT_HEADS = HEADS + 2 * KV_HEADS
HALF_JOINT = JOINT_HEADS // CORES
HALF_HEADS = HEADS // CORES
MESH = pl.DeviceIdType.MESH
F32, BF16 = jnp.float32, jnp.bfloat16


def chip_of(i, count):
    return (CHIPS * i) // count


def tile_of(chip, count):
    i = lax.div(count * chip + CHIPS - 1, CHIPS)
    ok = jnp.logical_and(i < count, lax.div(CHIPS * i, count) == chip)
    return jnp.minimum(i, count - 1), ok


def lanes_of(n):
    return pl.ds(pl.multiple_of(n * LANES, LANES), LANES)


def send(src, dst, send_sem, recv_sem, device):
    copy = pltpu.make_async_remote_copy(
        src_ref=src,
        dst_ref=dst,
        send_sem=send_sem,
        recv_sem=recv_sem,
        device_id={"seq": device},
        device_id_type=MESH,
    )
    copy.start()


def wait_bytes(ref, sem):
    pltpu.make_async_copy(ref, ref, sem).wait()


def cut_pieces(tiles, width, count):
    lane = lax.broadcasted_iota(jnp.int32, (ROWS, LANES), 1)
    pieces = []
    for j in range(count):
        t, off = divmod(width * j, LANES)
        piece = tiles[t] if off == 0 else pltpu.roll(tiles[t], LANES - off, 1)
        if off + width > LANES:
            rest = pltpu.roll(tiles[t + 1], LANES - off, 1)
            piece = jnp.where(lane < LANES - off, piece, rest)
        pieces.append(piece)
    return pieces


def join_pieces(pieces, width, tiles):
    lane = lax.broadcasted_iota(jnp.int32, (ROWS, LANES), 1)
    out = [None] * tiles

    def put(t, value):
        out[t] = value if out[t] is None else out[t] + value

    for j, piece in enumerate(pieces):
        t, off = divmod(width * j, LANES)
        moved = piece if off == 0 else pltpu.roll(piece, off, 1)
        if off + width > LANES:
            put(t, jnp.where(lane >= off, moved, 0.0))
            put(t + 1, jnp.where(lane < off, moved, 0.0))
        else:
            put(t, moved)
    return out


def kernel(
    ids_ref, len_ref, freq_ref, table_hbm, gain_ref, wqkv_hbm, bias_ref, keys_hbm, values_hbm,
    wout_hbm, mgain_ref, wgate_hbm, wup_hbm, wdown_hbm,
    att_ref, lay_ref,
    table, wqkv, keys, values, wout, wgate, wup, wdown,
    rows_f, n1s, n1r, t1s, t1r, n2s, n2r, t2s, t2r, cosr, sinr,
    part, bx, bs, br, jflat,
    ob, cx, cs, cr, aflat, tmp, ds_, dx, mb, nflat,
    es, er, e2s, e2r, dummy,
    tsem, wsem, ssem, rsem,
):
    me = lax.axis_index("seq")
    x = lax.div(me, PLANE)
    j0 = lax.rem(me, PLANE)
    chip = lax.div(me, CORES)
    c = lax.rem(me, CORES)
    other = me + 1 - 2 * c
    width = lay_ref.shape[1]
    block = PLANE * width
    tiles = block // LANES
    vocab_rows = table.shape[0]

    x_peers = [(k, lax.rem(x + k, XS)) for k in range(1, XS)]
    j_peers = [(k, lax.rem(j0 + k, PLANE)) for k in range(1, PLANE)]

    loads = []
    for k in range(XS):
        at = pl.ds(k * block, block)
        loads.append(pltpu.make_async_copy(table_hbm.at[:, at], table.at[:, at], tsem.at[k]))
        loads[-1].start()
    barrier = pltpu.get_barrier_semaphore()
    for _, p in x_peers:
        pl.semaphore_signal(barrier, inc=1, device_id={"seq": p * PLANE + j0}, device_id_type=MESH)
    for _, p in j_peers:
        pl.semaphore_signal(barrier, inc=1, device_id={"seq": x * PLANE + p}, device_id_type=MESH)
    weights = [
        pltpu.make_async_copy(src, dst, wsem.at[k])
        for k, (src, dst) in enumerate(
            [(wqkv_hbm, wqkv), (keys_hbm, keys), (values_hbm, values), (wout_hbm, wout),
             (wgate_hbm, wgate), (wup_hbm, wup), (wdown_hbm, wdown)]
        )
    ]
    for w in weights:
        w.start()

    lane = lax.broadcasted_iota(jnp.int32, (ROWS, LANES), 1)
    row = lax.broadcasted_iota(jnp.int32, (ROWS, LANES), 0)
    prompts = len_ref.shape[0]

    local = jnp.full((ROWS, vocab_rows), -1, jnp.int32)
    vrow = lax.broadcasted_iota(jnp.int32, (ROWS, vocab_rows), 0)
    vcol = lax.broadcasted_iota(jnp.int32, (ROWS, vocab_rows), 1)
    for r in range(ROWS):
        local = jnp.where(vrow == r, ids_ref[r % prompts, r // prompts] - me * vocab_rows, local)
    chosen = jnp.where(local == vcol, 1.0, 0.0).astype(BF16)
    square = jnp.zeros((ROWS, LANES), F32)
    for k in range(XS):
        loads[k].wait()
        found = jnp.dot(chosen, table[:, k * block : (k + 1) * block], preferred_element_type=F32)
        rows_f[:, k * block : (k + 1) * block] = found
        t1s[k] = found.astype(BF16)
        for t in range(tiles):
            v = found[:, t * LANES : (t + 1) * LANES]
            square = square + v * v
    scale = lax.rsqrt(jnp.sum(square, axis=-1, keepdims=True) / (XS * block) + NORM_EPS)
    gain = gain_ref[...].astype(F32)
    for k in range(XS):
        for t in range(tiles):
            g = k * tiles + t
            v = rows_f[:, g * LANES : (g + 1) * LANES] * scale * gain[g : g + 1, :]
            n1s[k, :, t * LANES : (t + 1) * LANES] = v.astype(BF16)

    pl.semaphore_wait(barrier, XS + PLANE - 2)

    for k, p in x_peers:
        send(n1s.at[p], n1r.at[k - 1], ssem.at[0], rsem.at[0], p * PLANE + j0)
    for k, p in x_peers:
        send(t1s.at[p], t1r.at[k - 1], ssem.at[1], rsem.at[1], p * PLANE + j0)

    place = jnp.zeros((ROWS, LANES), jnp.int32)
    for r in range(ROWS):
        place = jnp.where(row == r, len_ref[r % prompts] + r // prompts, place)
    angle = place.astype(F32) * freq_ref[...]
    cosr[...] = jnp.cos(angle)
    sine = jnp.sin(angle)
    sinr[...] = jnp.where(lane < HEAD_DIM // 2, -sine, sine)

    def gather_block(own, got):
        total = own[x].astype(F32)
        for k in range(XS - 1):
            total = total + got[k].astype(F32)
        return [total[:, t * LANES : (t + 1) * LANES] for t in range(tiles)]

    wait_bytes(n1r, rsem.at[0])
    for j, piece in enumerate(cut_pieces(gather_block(n1s, n1r), width, PLANE)):
        n2s[j] = piece
    for k, p in j_peers:
        send(n2s.at[p], n2r.at[k - 1], ssem.at[2], rsem.at[2], x * PLANE + p)
    wait_bytes(t1r, rsem.at[1])
    for j, piece in enumerate(cut_pieces(gather_block(t1s, t1r), width, PLANE)):
        t2s[j] = piece
    for k, p in j_peers:
        send(t2s.at[p], t2r.at[k - 1], ssem.at[3], rsem.at[3], x * PLANE + p)
    weights[0].wait()
    wait_bytes(n2r, rsem.at[2])
    normed = n2s[j0] + jnp.sum(n2r[...], axis=0)
    normed = normed[:, :width].astype(BF16)

    per = JOINT_HEADS // XS
    for k in range(XS):
        got = jnp.dot(
            normed, wqkv[:, k * per * LANES : (k + 1) * per * LANES], preferred_element_type=F32
        )
        for t in range(per):
            part[k * per + t] = got[:, t * LANES : (t + 1) * LANES]
    send(part.at[pl.ds(HALF_JOINT * (1 - c), HALF_JOINT)], bx, ssem.at[4], rsem.at[4], other)
    wait_bytes(bx, rsem.at[4])
    bs[...] = part[pl.ds(HALF_JOINT * c, HALF_JOINT)] + bx[...]
    for i in range(HALF_JOINT):
        p = chip_of(i, HALF_JOINT)

        @pl.when(chip != p)
        def _(i=i, p=p):
            slot = lax.rem(chip - p + CHIPS, CHIPS) - 1
            send(bs.at[i], br.at[slot], ssem.at[5], rsem.at[5], p * CORES + c)

    ib, b_on = tile_of(chip, HALF_JOINT)
    hb = HALF_JOINT * c + ib

    @pl.when(b_on)
    def _():
        wait_bytes(br, rsem.at[5])
        total = bs[ib] + jnp.sum(br[...], axis=0) + bias_ref[pl.ds(hb, 1), :]
        joint = total.astype(BF16).astype(F32)
        turned = joint * cosr[...] + pltpu.roll(joint, HEAD_DIM // 2, 1) * sinr[...]
        turn = jnp.where(hb < HEADS + KV_HEADS, 1.0, 0.0)
        jflat[:, lanes_of(hb)] = jnp.where(turn > 0.5, turned, joint).astype(BF16)

        @pl.loop(1, GROUP)
        def _(k):
            at = jflat.at[:, lanes_of(hb)]
            send(at, at, ssem.at[6], rsem.at[6], lax.rem(me + k, GROUP))

        wait_bytes(jflat.at[:, : (JOINT_HEADS - 1) * LANES], rsem.at[6])

    @pl.when(jnp.logical_not(b_on))
    def _():
        wait_bytes(jflat, rsem.at[6])

    weights[1].wait()
    weights[2].wait()
    group = HEADS // KV_HEADS
    span = keys.shape[1]
    lines = group * ROWS
    wide_row = lax.broadcasted_iota(jnp.int32, (lines, span), 0)
    even = lax.rem(wide_row, prompts) == 0
    where = me * span + lax.broadcasted_iota(jnp.int32, (lines, span), 1)
    valid = where < jnp.where(even, len_ref[0], len_ref[1])
    score_scale = 1.0 / math.sqrt(HEAD_DIM)
    nt = (((1,), (1,)), ((), ()))
    for k in range(KV_HEADS):
        at = slice(k * LANES, (k + 1) * LANES)
        query = jnp.concatenate(
            [
                jflat[:, h * LANES : (h + 1) * LANES].astype(F32)
                for h in range(k * group, (k + 1) * group)
            ],
            axis=0,
        ).astype(BF16)
        score = [
            lax.dot_general(query, keys[b, :, at], nt, preferred_element_type=F32)
            for b in range(prompts)
        ]
        score = jnp.where(valid, jnp.where(even, score[0], score[1]) * score_scale, MASKED)
        top = jnp.max(score, axis=-1, keepdims=True)
        weight = jnp.where(valid, jnp.exp(score - top), 0.0)
        total = jnp.sum(weight, axis=-1, keepdims=True)
        summed = jnp.dot(
            jnp.where(even, weight, 0.0).astype(BF16), values[0, :, at], preferred_element_type=F32
        ) + jnp.dot(
            jnp.where(even, 0.0, weight).astype(BF16), values[1, :, at], preferred_element_type=F32
        )
        top = jnp.broadcast_to(top, (lines, LANES))
        total = jnp.broadcast_to(total, (lines, LANES))
        for g in range(group):
            h = k * group + g
            ob[h, 0] = summed[g * ROWS : (g + 1) * ROWS]
            ob[h, 1] = top[g * ROWS : (g + 1) * ROWS]
            ob[h, 2] = total[g * ROWS : (g + 1) * ROWS]

    send(ob.at[pl.ds(HALF_HEADS * (1 - c), HALF_HEADS)], cx, ssem.at[7], rsem.at[7], other)
    wait_bytes(cx, rsem.at[7])
    for i in range(HALF_HEADS):
        h = HALF_HEADS * c + i
        top_a, top_b = ob[h, 1], cx[i, 1]
        top = jnp.maximum(top_a, top_b)
        scale_a, scale_b = jnp.exp(top_a - top), jnp.exp(top_b - top)
        cs[i, 0] = ob[h, 0] * scale_a + cx[i, 0] * scale_b
        cs[i, 1] = jnp.where(lane < LANES // 2, top, ob[h, 2] * scale_a + cx[i, 2] * scale_b)
    for i in range(HALF_HEADS):
        p = chip_of(i, HALF_HEADS)

        @pl.when(chip != p)
        def _(i=i, p=p):
            slot = lax.rem(chip - p + CHIPS, CHIPS) - 1
            send(cs.at[i], cr.at[slot], ssem.at[8], rsem.at[8], p * CORES + c)

    ic, c_on = tile_of(chip, HALF_HEADS)
    hc = HALF_HEADS * c + ic

    @pl.when(c_on)
    def _():
        kv = lax.div(hc, group)
        query = jflat[:, lanes_of(hc)]
        new_key = jflat[:, lanes_of(HEADS + kv)]
        new_value = jflat[:, lanes_of(HEADS + KV_HEADS + kv)]
        small_r = lax.broadcasted_iota(jnp.int32, (ROWS, ROWS), 0)
        small_c = lax.broadcasted_iota(jnp.int32, (ROWS, ROWS), 1)
        seen = jnp.logical_and(
            small_c <= small_r, lax.rem(small_c, prompts) == lax.rem(small_r, prompts)
        )
        score = lax.dot_general(query, new_key, nt, preferred_element_type=F32) * score_scale
        score = jnp.where(seen, score, MASKED)
        top = jnp.max(score, axis=-1, keepdims=True)
        weight = jnp.where(seen, jnp.exp(score - top), 0.0)
        total = jnp.sum(weight, axis=-1, keepdims=True)
        new_sum = jnp.dot(weight.astype(BF16), new_value, preferred_element_type=F32)
        low = lane < LANES // 2
        new_stat = jnp.where(
            low, jnp.broadcast_to(top, (ROWS, LANES)), jnp.broadcast_to(total, (ROWS, LANES))
        )
        wait_bytes(cr, rsem.at[8])
        stats = [new_stat, cs[ic, 1]] + [cr[s, 1] for s in range(CHIPS - 1)]
        sums = [new_sum, cs[ic, 0]] + [cr[s, 0] for s in range(CHIPS - 1)]
        best = functools.reduce(jnp.maximum, stats)
        acc = jnp.zeros((ROWS, LANES), F32)
        den = jnp.zeros((ROWS, LANES), F32)
        for stat, value in zip(stats, sums):
            scale = jnp.exp(stat - best)
            scale = jnp.where(low, scale, pltpu.roll(scale, LANES // 2, 1))
            acc = acc + value * scale
            den = den + stat * scale
        den = jnp.where(low, pltpu.roll(den, LANES // 2, 1), den)
        aflat[:, lanes_of(hc)] = (acc / den).astype(BF16)

        @pl.loop(1, GROUP)
        def _(k):
            at = aflat.at[:, lanes_of(hc)]
            send(at, at, ssem.at[9], rsem.at[9], lax.rem(me + k, GROUP))

        wait_bytes(aflat.at[:, : (HEADS - 1) * LANES], rsem.at[9])

    @pl.when(jnp.logical_not(c_on))
    def _():
        wait_bytes(aflat, rsem.at[9])

    weights[3].wait()
    attended = aflat[...]
    tmp[...] = jnp.zeros((ROWS, LANES), F32)
    tmp[:, :width] = lax.dot_general(attended, wout[...], nt, preferred_element_type=F32)
    wait_bytes(t2r, rsem.at[3])
    stream = t2s[j0] + jnp.sum(t2r[...], axis=0)
    mid = jnp.where(lane < width, tmp[...] + stream, 0.0)
    mine = jnp.where(lax.rem(row * 0 + c, CORES) == 0, mid, pltpu.roll(mid, width, 1))
    ds_[...] = mine
    send(ds_, dx, ssem.at[10], rsem.at[10], other)
    wait_bytes(dx, rsem.at[10])
    mb[chip] = mine + dx[...]

    @pl.loop(1, CHIPS)
    def _(k):
        to = lax.rem(chip + k, CHIPS)
        send(mb.at[chip], mb.at[chip], ssem.at[11], rsem.at[11], to * CORES + c)

    att_ref[...] = attended
    weights[4].wait()
    weights[5].wait()
    weights[6].wait()
    wait_bytes(mb.at[pl.ds(0, CHIPS - 1)], rsem.at[11])
    mids = join_pieces([mb[p] for p in range(CHIPS)], CORES * width, XS * tiles)
    square = jnp.zeros((ROWS, LANES), F32)
    for v in mids:
        square = square + v * v
    scale = lax.rsqrt(jnp.sum(square, axis=-1, keepdims=True) / (XS * block) + NORM_EPS)
    gain = mgain_ref[...].astype(F32)
    for g, v in enumerate(mids):
        nflat[:, g * LANES : (g + 1) * LANES] = (v * scale * gain[g : g + 1, :]).astype(BF16)
    normed_mid = nflat[...]
    gate = jnp.dot(normed_mid, wgate[...], preferred_element_type=F32)
    upper = jnp.dot(normed_mid, wup[...], preferred_element_type=F32)
    hidden = (gate / (1.0 + jnp.exp(-gate)) * upper).astype(BF16)
    for k in range(XS):
        es[k] = jnp.dot(
            hidden, wdown[:, k * block : (k + 1) * block], preferred_element_type=F32
        )
    for k, p in x_peers:
        send(es.at[p], er.at[k - 1], ssem.at[12], rsem.at[12], p * PLANE + j0)
    wait_bytes(er, rsem.at[12])
    for j, piece in enumerate(cut_pieces(gather_block(es, er), width, PLANE)):
        e2s[j] = piece
    for k, p in j_peers:
        send(e2s.at[p], e2r.at[k - 1], ssem.at[13], rsem.at[13], x * PLANE + p)
    wait_bytes(e2r, rsem.at[13])
    final = mid + e2s[j0] + jnp.sum(e2r[...], axis=0)
    lay_ref[...] = final[:, :width].astype(BF16)

    for sem, ref in (
        (0, n1r), (1, t1r), (2, n2r), (3, t2r), (4, bx), (7, cx), (10, dx), (12, er), (13, e2r),
    ):
        wait_bytes(ref, ssem.at[sem])
    wait_bytes(mb.at[pl.ds(0, CHIPS - 1)], ssem.at[11])
    @pl.when(b_on)
    def _():
        wait_bytes(bs.at[pl.ds(0, HALF_JOINT - 1)], ssem.at[5])
        wait_bytes(dummy, ssem.at[6])

    @pl.when(jnp.logical_not(b_on))
    def _():
        wait_bytes(bs, ssem.at[5])

    @pl.when(c_on)
    def _():
        wait_bytes(cs.at[pl.ds(0, HALF_HEADS - 1)], ssem.at[8])
        wait_bytes(dummy, ssem.at[9])

    @pl.when(jnp.logical_not(c_on))
    def _():
        wait_bytes(cs, ssem.at[8])


def body(
    token_ids, lengths, embed_table, attn_gain, w_qkv, qkv_bias, cache_keys, cache_values, w_out,
    mlp_gain, w_gate, w_up, w_down,
):
    steps, prompts = token_ids.shape
    vocab_rows, model = embed_table.shape
    width = w_out.shape[1]
    block = PLANE * width
    half = HEAD_DIM // 2
    frequency = np.float32(ROPE_BASE) ** (
        np.float32(-2.0) * np.arange(half, dtype=np.float32) / np.float32(HEAD_DIM)
    )
    frequency = jnp.asarray(np.tile(np.concatenate([frequency, frequency]), (ROWS, 1)), F32)
    vmem = pl.BlockSpec(memory_space=pltpu.VMEM)
    smem = pl.BlockSpec(memory_space=pltpu.SMEM)
    hbm = pl.BlockSpec(memory_space=pl.ANY)
    w_out_t = w_out.T

    def like(a):
        return pltpu.VMEM(a.shape, a.dtype)

    def tile(*lead, dtype=F32):
        return pltpu.VMEM((*lead, ROWS, LANES), dtype)

    def wide(*lead, dtype):
        return pltpu.VMEM((*lead, ROWS, block), dtype)

    attended, layer_out = pl.pallas_call(
        kernel,
        out_shape=(
            jax.ShapeDtypeStruct((ROWS, HEADS * HEAD_DIM), BF16),
            jax.ShapeDtypeStruct((ROWS, width), BF16),
        ),
        in_specs=[smem, smem, vmem, hbm, vmem, hbm, vmem, hbm, hbm, hbm, vmem, hbm, hbm, hbm],
        out_specs=(vmem, vmem),
        scratch_shapes=[
            like(embed_table), like(w_qkv), like(cache_keys), like(cache_values), like(w_out_t),
            like(w_gate), like(w_up), like(w_down),
            pltpu.VMEM((ROWS, model), F32),
            wide(XS, dtype=BF16), wide(XS - 1, dtype=BF16),
            wide(XS, dtype=BF16), wide(XS - 1, dtype=BF16),
            tile(PLANE), tile(PLANE - 1), tile(PLANE), tile(PLANE - 1), tile(), tile(),
            tile(JOINT_HEADS), tile(HALF_JOINT), tile(HALF_JOINT), tile(CHIPS - 1),
            pltpu.VMEM((ROWS, JOINT_HEADS * LANES), BF16),
            tile(HEADS, 3), tile(HALF_HEADS, 3), tile(HALF_HEADS, 2), tile(CHIPS - 1, 2),
            pltpu.VMEM((ROWS, HEADS * LANES), BF16),
            tile(), tile(), tile(), tile(CHIPS),
            pltpu.VMEM((ROWS, model), BF16),
            wide(XS, dtype=F32), wide(XS - 1, dtype=F32), tile(PLANE), tile(PLANE - 1),
            tile(GROUP - 1, dtype=BF16),
            pltpu.SemaphoreType.DMA((XS,)),
            pltpu.SemaphoreType.DMA((7,)),
            pltpu.SemaphoreType.DMA((14,)),
            pltpu.SemaphoreType.DMA((14,)),
        ],
        compiler_params=pltpu.CompilerParams(
            collective_id=0, has_side_effects=True, vmem_limit_bytes=60 * 2**20
        ),
        name="layer",
    )(
        token_ids.T, lengths, frequency, embed_table, attn_gain.reshape(-1, LANES), w_qkv,
        qkv_bias.reshape(-1, LANES), cache_keys, cache_values, w_out_t,
        mlp_gain.reshape(-1, LANES), w_gate, w_up, w_down,
    )
    return (
        attended.reshape(steps, prompts, -1),
        layer_out.reshape(steps, prompts, width),
    )


def solution(mesh):
    return jax.shard_map(
        body,
        mesh=mesh,
        in_specs=(
            P(None, "parts"), P("parts"), P("seq", None), P(), P("seq", None), P(),
            P("parts", "seq", None), P("parts", "seq", None), P(None, "seq"), P(),
            P(None, "seq"), P(None, "seq"), P("seq", None),
        ),
        out_specs=(P(None, "parts", None), P(None, "parts", "seq")),
        check_vma=False,
    )
```

time: 718 us -> 107 us (0.15); the launches traced: 707 us -> 106 us
  waiting for transfers between devices: 551 us -> 0 us
  Pallas kernels: 0 us -> 103 us
  blocking collectives: 87.5 us -> 0 us
  local copies, waits for them, and re-layouts: 25.4 us -> 2.82 us
  other arithmetic: 19.2 us -> 0 us
  between operations: 16 us -> 0.64 us
  matrix products: 7.37 us -> 0 us
    psum x2 -> x0, waiting for transfers between devices: 380 us -> none  [the longest x1 199 us: body(): stream = lax.psum(partial_rows, SEQ)]
    pallas_call x0 -> x1, Pallas kernels: none -> 103 us  [body(): pl.pallas_call(kernel, out_shape=(jax.ShapeDtypeStruct((ROWS, HEADS * HEA...]
    unnamed x8 -> x0, waiting for transfers between devices: 100 us -> none
    all_gather x2 -> x0, waiting for transfers between devices: 71.1 us -> none  [gathered_once(): both, at, found = (lax.all_gather(jnp.concatenate(lines), axis), 0, {})]
    all_gather x2 -> x0, blocking collectives: 64.8 us -> none  [the longest x1 57.3 us: body(): mid_rows = lax.all_gather(mid_shard, SEQ, axis=2, tiled=True)]
    unnamed x1 -> x0, blocking collectives: 22.6 us -> none
    reduce_sum x3 -> x0, other arithmetic: 8.31 us -> none  [the longest x2 8.13 us: rms_normalize(): mean_square = jnp.mean(rows * rows, axis=-1, keepdims=True)]
    dot_general x8 -> x0, matrix products: 7.37 us -> none  [the longest x1 1.87 us: body(): jnp.dot(hidden, w_down, preferred_element_type=jnp.float32)]
  transfers between devices with their start and end apart: 6 -> 0, of which waited for: 6 -> 0; matrix products, arithmetic and copies ran while one was open for 1% -> 0% of each run, Pallas kernels for 0% -> 0%
where the time goes in v1:
time: 107 us; the launch traced here: 106 us
  Pallas kernels  103 us (96%)
  local copies, waits for them, and re-layouts  2.82 us (3%)
    pallas_call x1, Pallas kernels, body(): pl.pallas_call(kernel, out_shape=(jax.ShapeDtypeStruct((ROWS, HEADS * HEA...  103 us

profile of v1, /device:TPU:513, one launch (start us, length us, event | category | flops | bytes accessed | tf_op | source)
XLA Modules:
  0.0 106.5 jit_solution(11394653550509304105)
XLA Ops:
  0.6 103.0 %layer.1 = (bf16[8,5120]{1,0:T(8,128)(2,1)}, bf16[8,40]{1,0:T(8,128)(2,1)}) custom-call(s32[2,4]{1,0:T(2,128)} %bitcast.11, s32[2]{0:T(128)} %len_ref.1, f32[8,128]{1,0:T(8,128)} %constant.2.clone.freq_ref, bf16[594,5120]{1,0:T(8,128)(2,1)} %table_hbm.1, bf16[40,128]{1,0:T(8,128)(2,1)} %bitcast.8, bf16[40,7168]{1,0:T(8,128)(2,1)} %wqkv_hbm.1, ...), custom_call_target="tpu_custom_call" | custom-call | tf_op jit(solution)/shard_map/layer/pallas_call | solution.py:450
  103.7 1.6 %reshape.22 = bf16[4,2,5120]{2,1,0:T(2,128)(2,1)} reshape(bf16[8,5120]{1,0:T(8,128)(2,1)} %get-tuple-element.4) | data formatting | bytes 163840 | tf_op jit(solution)/shard_map/reshape | solution.py:488
  105.2 1.3 %copy.17 = bf16[4,2,40]{2,1,0:T(2,128)(2,1)} copy(bf16[4,2,40]{2,1,0:T(2,128)(2,1)} %bitcast.10) | data formatting | bytes 1280

commit v2 on v1

v2 whole, which is shorter than its diff:
```python
import functools
import math

import jax
import jax.numpy as jnp
import numpy as np
from jax import lax
from jax.experimental import pallas as pl
from jax.experimental.pallas import tpu as pltpu
from jax.sharding import PartitionSpec as P

HEADS = 40
KV_HEADS = 8
HEAD_DIM = 128
NORM_EPS = 1e-06
ROPE_BASE = 1000000.0
MASKED = -1e30

ROWS = 8
LANES = 128
XS, YS, CORES = 8, 8, 2
PLANE = YS * CORES
CHIPS = XS * YS
GROUP = CHIPS * CORES
JOINT_HEADS = HEADS + 2 * KV_HEADS
HALF_JOINT = JOINT_HEADS // CORES
GROUPS = KV_HEADS // CORES
UNITS = JOINT_HEADS // KV_HEADS
JOINT_AT = (0, 2, 4, 6, 9, 11, 13)
HEAD_AT = (4, 6, 0, 2, 13)
FAR_FIRST = (4, 3, 5, 2, 6, 1, 7, 0)
HALF_HEADS = HEADS // CORES
MESH = pl.DeviceIdType.MESH
F32, BF16 = jnp.float32, jnp.bfloat16


def position(within, places):
    at, ok = 0, False
    for r, p in enumerate(places):
        at = jnp.where(within == p, r, at)
        ok = jnp.logical_or(ok, within == p)
    return at, ok


def own_gain(gain, me, width):
    start = me * width
    tile, off = lax.div(start, LANES), lax.rem(start, LANES)
    line = lax.broadcasted_iota(jnp.int32, gain.shape, 0)
    lane = lax.broadcasted_iota(jnp.int32, (1, LANES), 1)
    first = jnp.sum(jnp.where(line == tile, gain, 0.0), axis=0, keepdims=True)
    second = jnp.sum(jnp.where(line == tile + 1, gain, 0.0), axis=0, keepdims=True)
    both = jnp.where(lane >= off, first, second)
    return pltpu.roll(jnp.broadcast_to(both, (ROWS, LANES)), lax.rem(LANES - off, LANES), 1)


def lanes_of(n):
    return pl.ds(pl.multiple_of(n * LANES, LANES), LANES)


def send(src, dst, send_sem, recv_sem, device):
    copy = pltpu.make_async_remote_copy(
        src_ref=src,
        dst_ref=dst,
        send_sem=send_sem,
        recv_sem=recv_sem,
        device_id={"seq": device},
        device_id_type=MESH,
    )
    copy.start()


def packed(value, level):
    lane = lax.broadcasted_iota(jnp.int32, (ROWS, LANES), 1)
    first = level.astype(BF16).astype(F32)
    second = (level - first).astype(BF16).astype(F32)
    third = level - first - second
    quarter = LANES // 4
    parts = jnp.where(
        lane < quarter, first,
        jnp.where(lane < 2 * quarter, second, jnp.where(lane < 3 * quarter, third, 0.0)),
    )
    return jnp.concatenate([value, parts], axis=0).astype(BF16)


def wait_bytes(ref, sem):
    pltpu.make_async_copy(ref, ref, sem).wait()


def cut_pieces(tiles, width, count):
    lane = lax.broadcasted_iota(jnp.int32, (ROWS, LANES), 1)
    pieces = []
    for j in range(count):
        t, off = divmod(width * j, LANES)
        piece = tiles[t] if off == 0 else pltpu.roll(tiles[t], LANES - off, 1)
        if off + width > LANES:
            rest = pltpu.roll(tiles[t + 1], LANES - off, 1)
            piece = jnp.where(lane < LANES - off, piece, rest)
        pieces.append(piece)
    return pieces


def join_pieces(pieces, width, tiles):
    lane = lax.broadcasted_iota(jnp.int32, (ROWS, LANES), 1)
    out = [None] * tiles

    def put(t, value):
        out[t] = value if out[t] is None else out[t] + value

    for j, piece in enumerate(pieces):
        t, off = divmod(width * j, LANES)
        moved = piece if off == 0 else pltpu.roll(piece, off, 1)
        if off + width > LANES:
            put(t, jnp.where(lane >= off, moved, 0.0))
            put(t + 1, jnp.where(lane < off, moved, 0.0))
        else:
            put(t, moved)
    return out


def kernel(
    ids_ref, len_ref, freq_ref, table_hbm, gain_ref, wqkv_hbm, bias_ref, keys_hbm, values_hbm,
    wout_hbm, mgain_ref, wgate_hbm, wup_hbm, wdown_hbm,
    att_ref, lay_ref,
    table, wqkv, keys, values, wout, wgate, wup, wdown,
    a1s, a1r, q1s, q1r, a2s, a2r, cosr, sinr,
    po, bx, bs, br, jflat,
    oo, ow, cx, cs, cr, levels, aflat, tmp, ds_, dx, mb, nflat,
    es, er, e2s, e2r, dummy,
    tsem, wsem, ssem, rsem, bxsem, jsem, cxsem,
):
    me = lax.axis_index("seq")
    x = lax.div(me, PLANE)
    j0 = lax.rem(me, PLANE)
    y = lax.div(j0, CORES)
    chip = lax.div(me, CORES)
    c = lax.rem(me, CORES)
    other = me + 1 - 2 * c
    width = lay_ref.shape[1]
    block = PLANE * width
    tiles = block // LANES
    vocab_rows = table.shape[1]
    group = HEADS // KV_HEADS

    x_peers = [(k, lax.rem(x + k, XS)) for k in FAR_FIRST[:-1]]
    y_part = [lax.rem(y + k, YS) * CORES for k in range(YS)]
    x_part = [lax.rem(x + k, XS) * PLANE for k in range(XS)]
    plane_peers = [
        (k, e, y_part[k] + lax.rem(c + e, CORES))
        for k in FAR_FIRST for e in range(CORES) if k or e
    ]
    chip_peers = sorted(
        [(i, j) for i in range(XS) for j in range(YS) if i or j],
        key=lambda p: -min(p[0], XS - p[0]) - min(p[1], YS - p[1]),
    )

    def to_all(tile, send_sem, recv_sem):
        for i, j in chip_peers:
            for e in range(CORES):
                send(tile, tile, send_sem, recv_sem, x_part[i] + y_part[j] + e)
        send(tile, tile, send_sem, recv_sem, other)

    barrier = pltpu.get_barrier_semaphore()
    for _, p in x_peers:
        pl.semaphore_signal(barrier, inc=1, device_id={"seq": p * PLANE + j0}, device_id_type=MESH)
    for _, _, p in plane_peers:
        pl.semaphore_signal(barrier, inc=1, device_id={"seq": x * PLANE + p}, device_id_type=MESH)
    order = [p for _, p in x_peers] + [x]
    loads = []
    for k, p in enumerate(order):
        at = pl.ds(pl.multiple_of(p * block, LANES), block)
        loads.append(pltpu.make_async_copy(table_hbm.at[:, at], table.at[k], tsem.at[k]))
        loads[-1].start()
    weights = [
        pltpu.make_async_copy(src, dst, wsem.at[k])
        for k, (src, dst) in enumerate(
            [(wqkv_hbm, wqkv), (keys_hbm, keys), (values_hbm, values), (wout_hbm, wout),
             (wgate_hbm, wgate), (wup_hbm, wup), (wdown_hbm, wdown)]
        )
    ]
    for w in weights:
        w.start()

    lane = lax.broadcasted_iota(jnp.int32, (ROWS, LANES), 1)
    row = lax.broadcasted_iota(jnp.int32, (ROWS, LANES), 0)
    low = lane < LANES // 2
    prompts = len_ref.shape[0]

    local = jnp.full((ROWS, vocab_rows), -1, jnp.int32)
    vrow = lax.broadcasted_iota(jnp.int32, (ROWS, vocab_rows), 0)
    vcol = lax.broadcasted_iota(jnp.int32, (ROWS, vocab_rows), 1)
    for r in range(ROWS):
        local = jnp.where(vrow == r, ids_ref[r % prompts, r // prompts] - me * vocab_rows, local)
    chosen = jnp.where(local == vcol, 1.0, 0.0).astype(BF16)
    square = jnp.zeros((ROWS, LANES), F32)
    for k in range(XS):
        loads[k].wait()
        found = jnp.dot(chosen, table[k], preferred_element_type=F32)
        a1s[k] = found.astype(BF16)
        for t in range(tiles):
            v = found[:, t * LANES : (t + 1) * LANES]
            square = square + v * v
        if k == 0:
            pl.semaphore_wait(barrier, XS + PLANE - 2)
        if k < XS - 1:
            d, p = x_peers[k]
            send(a1s.at[k], a1r.at[d - 1], ssem.at[0], rsem.at[0], p * PLANE + j0)
    q1s[...] = jnp.broadcast_to(
        jnp.sum(square, axis=-1, keepdims=True) / (XS * block), (ROWS, LANES)
    )
    for d, p in x_peers:
        send(q1s, q1r.at[d - 1], ssem.at[1], rsem.at[1], p * PLANE + j0)

    place = jnp.zeros((ROWS, LANES), jnp.int32)
    for r in range(ROWS):
        place = jnp.where(row == r, len_ref[r % prompts] + r // prompts, place)
    angle = place.astype(F32) * freq_ref[...]
    cosr[...] = jnp.cos(angle)
    sine = jnp.sin(angle)
    sinr[...] = jnp.where(lane < HEAD_DIM // 2, -sine, sine)

    wait_bytes(a1r, rsem.at[0])
    wait_bytes(q1r, rsem.at[1])
    total = a1s[XS - 1].astype(F32)
    for k in range(XS - 1):
        total = total + a1r[k].astype(F32)
    found = [total[:, t * LANES : (t + 1) * LANES] for t in range(tiles)]
    square = q1s[...] + jnp.sum(q1r[...], axis=0)
    for j, piece in enumerate(cut_pieces(found, width, PLANE)):
        a2s[j] = jnp.where(low, piece, square)
    for k, e, p in plane_peers:
        send(a2s.at[p], a2r.at[k * CORES + e - 1], ssem.at[2], rsem.at[2], x * PLANE + p)
    weights[0].wait()
    gain = own_gain(gain_ref[...].astype(F32), me, width)
    wait_bytes(a2r, rsem.at[2])
    stream = a2s[j0] + jnp.sum(a2r[...], axis=0)
    scale = lax.rsqrt(jnp.broadcast_to(stream[:, LANES - 1 :], (ROWS, LANES)) + NORM_EPS)
    normed = (stream * scale * gain).astype(BF16)[:, :width]

    half_group = lax.div(chip, CHIPS // GROUPS)
    within = lax.rem(chip, CHIPS // GROUPS)
    far_groups = [lax.rem(half_group + k, GROUPS) for k in (2, 1, 3, 0)]
    near_groups = [lax.rem(half_group + k, GROUPS) for k in (0, 1, 3, 2)]

    def project(side, g):
        starts = [
            (HALF_HEADS * side + group * g, group),
            (HEADS + GROUPS * side + g, 1),
            (HEADS + KV_HEADS + GROUPS * side + g, 1),
        ]
        out = []
        for at, n in starts:
            cols = pl.ds(pl.multiple_of(at * LANES, LANES), n * LANES)
            got = jnp.dot(normed, wqkv[:, cols], preferred_element_type=F32)
            out += [got[:, t * LANES : (t + 1) * LANES] for t in range(n)]
        return out

    for n, g in enumerate(far_groups):
        for r, v in enumerate(project(1 - c, g)):
            po[n, r] = v
        send(po.at[n], bx.at[n], ssem.at[4], bxsem.at[n], other)
    for n, g in enumerate(far_groups):
        mine = project(c, g)
        wait_bytes(bx.at[n], bxsem.at[n])
        for r in range(UNITS):
            bs[n, r] = mine[r] + bx[n, r]
        for r in range(UNITS):
            p = (CHIPS // GROUPS) * g + JOINT_AT[r]

            def go(n=n, r=r, p=p):
                slot = lax.rem(chip - p + CHIPS, CHIPS) - 1
                send(bs.at[n, r], br.at[slot], ssem.at[5], rsem.at[5], p * CORES + c)

            if n < GROUPS - 1:
                go()
            else:
                pl.when(within != JOINT_AT[r])(go)

    rb, b_on = position(within, JOINT_AT)
    nb = UNITS * (GROUPS * c + half_group) + rb

    @pl.when(b_on)
    def _():
        wait_bytes(br, rsem.at[5])
        at = jnp.where(
            rb < group, HALF_HEADS * c + group * half_group + rb,
            HEADS + GROUPS * c + half_group + jnp.where(rb > group, KV_HEADS, 0),
        )
        total = bs[GROUPS - 1, rb].astype(F32)
        for k in range(CHIPS - 1):
            total = total + br[k].astype(F32)
        total = total + bias_ref[pl.ds(at, 1), :]
        joint = total.astype(BF16).astype(F32)
        turned = joint * cosr[...] + pltpu.roll(joint, HEAD_DIM // 2, 1) * sinr[...]
        turn = jnp.where(rb <= group, 1.0, 0.0)
        jflat[:, lanes_of(nb)] = jnp.where(turn > 0.5, turned, joint).astype(BF16)
        tile = jflat.at[:, lanes_of(nb)]
        to_all(tile, ssem.at[6], jsem.at[GROUPS * c + half_group])

    weights[1].wait()
    weights[2].wait()
    span = keys.shape[1]
    lines = group * ROWS
    wide_row = lax.broadcasted_iota(jnp.int32, (lines, span), 0)
    even = lax.rem(wide_row, prompts) == 0
    where = me * span + lax.broadcasted_iota(jnp.int32, (lines, span), 1)
    valid = where < jnp.where(even, len_ref[0], len_ref[1])
    score_scale = 1.0 / math.sqrt(HEAD_DIM)
    nt = (((1,), (1,)), ((), ()))

    def attend(side, g, into):
        kv = GROUPS * side + g
        base = UNITS * kv
        at = lanes_of(kv)
        query = jnp.concatenate(
            [jflat[:, lanes_of(base + r)].astype(F32) for r in range(group)], axis=0
        ).astype(BF16)
        score = [
            lax.dot_general(query, keys[b, :, at], nt, preferred_element_type=F32)
            for b in range(prompts)
        ]
        score = jnp.where(valid, jnp.where(even, score[0], score[1]) * score_scale, MASKED)
        top = jnp.max(score, axis=-1, keepdims=True)
        weight = jnp.where(valid, jnp.exp(score - top), 0.0)
        total = jnp.sum(weight, axis=-1, keepdims=True)
        summed = jnp.dot(
            jnp.where(even, weight, 0.0).astype(BF16), values[0, :, at], preferred_element_type=F32
        ) + jnp.dot(
            jnp.where(even, 0.0, weight).astype(BF16), values[1, :, at], preferred_element_type=F32
        )
        top = jnp.broadcast_to(top, (lines, LANES))
        total = jnp.broadcast_to(total, (lines, LANES))
        for r in range(group):
            into[r, 0] = summed[r * ROWS : (r + 1) * ROWS]
            into[r, 1] = top[r * ROWS : (r + 1) * ROWS]
            into[r, 2] = total[r * ROWS : (r + 1) * ROWS]

    def joint_group(kv):
        return jflat.at[:, pl.ds(pl.multiple_of(kv * UNITS * LANES, LANES), UNITS * LANES)]

    def merge(n, g):
        wait_bytes(cx.at[n], cxsem.at[n])
        for r in range(group):
            top_a, top_b = ow[n, r, 1], cx[n, r, 1]
            top = jnp.maximum(top_a, top_b)
            scale_a, scale_b = jnp.exp(top_a - top), jnp.exp(top_b - top)
            summed = ow[n, r, 0] * scale_a + cx[n, r, 0] * scale_b
            total = ow[n, r, 2] * scale_a + cx[n, r, 2] * scale_b
            some = total > 0.0
            total = jnp.where(some, total, 1.0)
            level = jnp.where(some, top + jnp.log(total), MASKED)
            cs[n, r] = packed(jnp.where(some, summed / total, 0.0), level)
        across = lax.rem(g + GROUPS // 2, GROUPS)
        for r in range(group):
            p = (CHIPS // GROUPS) * across + HEAD_AT[r]

            def go(r=r, p=p):
                slot = lax.rem(chip - p + CHIPS, CHIPS) - 1
                send(cs.at[n, r], cr.at[slot], ssem.at[8], rsem.at[8], p * CORES + c)

            if n < GROUPS - 1:
                go()
            else:
                pl.when(within != HEAD_AT[r])(go)

    for n, g in enumerate(near_groups):
        kv = GROUPS * (1 - c) + g
        wait_bytes(joint_group(kv), jsem.at[kv])
        attend(1 - c, g, oo.at[n])
        send(oo.at[n], cx.at[n], ssem.at[7], cxsem.at[n], other)
        kv = GROUPS * c + g
        if n == 0:
            @pl.when(b_on)
            def _(kv=kv):
                part = pl.ds(pl.multiple_of(kv * UNITS * LANES, LANES), (UNITS - 1) * LANES)
                wait_bytes(jflat.at[:, part], jsem.at[kv])

            @pl.when(jnp.logical_not(b_on))
            def _(kv=kv):
                wait_bytes(joint_group(kv), jsem.at[kv])
        else:
            wait_bytes(joint_group(kv), jsem.at[kv])
        attend(c, g, ow.at[n])
        if n:
            merge(n - 1, near_groups[n - 1])
    merge(GROUPS - 1, near_groups[-1])

    rc, c_on = position(within, HEAD_AT)
    gc = lax.rem(half_group + GROUPS // 2, GROUPS)
    hc = HALF_HEADS * c + group * gc + rc

    @pl.when(c_on)
    def _():
        base = UNITS * (GROUPS * c + gc)
        query = jflat[:, lanes_of(base + rc)]
        new_key = jflat[:, lanes_of(base + group)]
        new_value = jflat[:, lanes_of(base + group + 1)]
        small_r = lax.broadcasted_iota(jnp.int32, (ROWS, ROWS), 0)
        small_c = lax.broadcasted_iota(jnp.int32, (ROWS, ROWS), 1)
        seen = jnp.logical_and(
            small_c <= small_r, lax.rem(small_c, prompts) == lax.rem(small_r, prompts)
        )
        score = lax.dot_general(query, new_key, nt, preferred_element_type=F32) * score_scale
        score = jnp.where(seen, score, MASKED)
        top = jnp.max(score, axis=-1, keepdims=True)
        weight = jnp.where(seen, jnp.exp(score - top), 0.0)
        total = jnp.sum(weight, axis=-1, keepdims=True)
        new_sum = jnp.dot(weight.astype(BF16), new_value, preferred_element_type=F32)
        best = top + jnp.log(total)
        levels[CHIPS] = jnp.broadcast_to(best, (ROWS, LANES))
        best = levels[CHIPS]
        wait_bytes(cr, rsem.at[8])

        def partial(s):
            return cs[GROUPS - 1, rc] if s == CHIPS - 1 else cr[s]

        for s in range(CHIPS):
            level = partial(s)[ROWS:].astype(F32)
            level = level + pltpu.roll(level, LANES // 2, 1)
            level = level + pltpu.roll(level, LANES // 4, 1)
            levels[s] = level
            best = jnp.maximum(best, level)
        den = jnp.exp(levels[CHIPS] - best)
        acc = new_sum / total * den
        for s in range(CHIPS):
            scale = jnp.exp(levels[s] - best)
            acc = acc + partial(s)[:ROWS].astype(F32) * scale
            den = den + scale
        aflat[:, lanes_of(hc)] = (acc / den).astype(BF16)
        to_all(aflat.at[:, lanes_of(hc)], ssem.at[9], rsem.at[9])
        wait_bytes(aflat.at[:, : (HEADS - 1) * LANES], rsem.at[9])

    @pl.when(jnp.logical_not(c_on))
    def _():
        wait_bytes(aflat, rsem.at[9])

    weights[3].wait()
    attended = aflat[...]
    tmp[...] = jnp.zeros((ROWS, LANES), F32)
    tmp[:, :width] = lax.dot_general(attended, wout[...], nt, preferred_element_type=F32)
    mid = jnp.where(lane < width, tmp[...] + stream, 0.0)
    mine = jnp.where(lax.rem(row * 0 + c, CORES) == 0, mid, pltpu.roll(mid, width, 1))
    ds_[...] = mine
    send(ds_, dx, ssem.at[10], rsem.at[10], other)
    wait_bytes(dx, rsem.at[10])
    mb[chip] = (mine + dx[...]).astype(BF16)
    for i, j in chip_peers:
        send(mb.at[chip], mb.at[chip], ssem.at[11], rsem.at[11], x_part[i] + y_part[j] + c)

    att_ref[...] = attended
    weights[4].wait()
    weights[5].wait()
    weights[6].wait()
    wait_bytes(mb.at[pl.ds(0, CHIPS - 1)], rsem.at[11])
    mids = join_pieces([mb[p].astype(F32) for p in range(CHIPS)], CORES * width, XS * tiles)
    square = jnp.zeros((ROWS, LANES), F32)
    for v in mids:
        square = square + v * v
    scale = lax.rsqrt(jnp.sum(square, axis=-1, keepdims=True) / (XS * block) + NORM_EPS)
    gain = mgain_ref[...].astype(F32)
    for g, v in enumerate(mids):
        nflat[:, g * LANES : (g + 1) * LANES] = (v * scale * gain[g : g + 1, :]).astype(BF16)
    normed_mid = nflat[...]
    gate = jnp.dot(normed_mid, wgate[...], preferred_element_type=F32)
    upper = jnp.dot(normed_mid, wup[...], preferred_element_type=F32)
    hidden = (gate / (1.0 + jnp.exp(-gate)) * upper).astype(BF16)
    for k, p in enumerate(order):
        at = pl.ds(pl.multiple_of(p * block, LANES), block)
        es[k] = jnp.dot(hidden, wdown[:, at], preferred_element_type=F32).astype(BF16)
        if k < XS - 1:
            d = x_peers[k][0]
            send(es.at[k], er.at[d - 1], ssem.at[12], rsem.at[12], p * PLANE + j0)
    wait_bytes(er, rsem.at[12])
    total = es[XS - 1].astype(F32)
    for k in range(XS - 1):
        total = total + er[k].astype(F32)
    found = [total[:, t * LANES : (t + 1) * LANES] for t in range(tiles)]
    for j, piece in enumerate(cut_pieces(found, width, PLANE)):
        e2s[j] = piece
    for k, e, p in plane_peers:
        send(e2s.at[p], e2r.at[k * CORES + e - 1], ssem.at[13], rsem.at[13], x * PLANE + p)
    wait_bytes(e2r, rsem.at[13])
    final = mid + e2s[j0] + jnp.sum(e2r[...], axis=0)
    lay_ref[...] = final[:, :width].astype(BF16)

    for sem, ref in (
        (0, a1r), (1, q1r), (2, a2r), (4, bx), (7, cx), (10, dx), (12, er), (13, e2r),
    ):
        wait_bytes(ref, ssem.at[sem])
    wait_bytes(mb.at[pl.ds(0, CHIPS - 1)], ssem.at[11])

    @pl.when(b_on)
    def _():
        wait_bytes(br.at[pl.ds(0, HALF_JOINT - 1)], ssem.at[5])
        wait_bytes(dummy, ssem.at[6])

    @pl.when(jnp.logical_not(b_on))
    def _():
        wait_bytes(br.at[pl.ds(0, HALF_JOINT)], ssem.at[5])

    @pl.when(c_on)
    def _():
        wait_bytes(cr.at[pl.ds(0, HALF_HEADS - 1)], ssem.at[8])
        wait_bytes(dummy, ssem.at[9])

    @pl.when(jnp.logical_not(c_on))
    def _():
        wait_bytes(cr.at[pl.ds(0, HALF_HEADS)], ssem.at[8])


def body(
    token_ids, lengths, embed_table, attn_gain, w_qkv, qkv_bias, cache_keys, cache_values, w_out,
    mlp_gain, w_gate, w_up, w_down,
):
    steps, prompts = token_ids.shape
    vocab_rows, model = embed_table.shape
    width = w_out.shape[1]
    block = PLANE * width
    per_group = HEADS // KV_HEADS
    half = HEAD_DIM // 2
    frequency = np.float32(ROPE_BASE) ** (
        np.float32(-2.0) * np.arange(half, dtype=np.float32) / np.float32(HEAD_DIM)
    )
    frequency = jnp.asarray(np.tile(np.concatenate([frequency, frequency]), (ROWS, 1)), F32)
    vmem = pl.BlockSpec(memory_space=pltpu.VMEM)
    smem = pl.BlockSpec(memory_space=pltpu.SMEM)
    hbm = pl.BlockSpec(memory_space=pl.ANY)
    w_out_t = w_out.T

    def like(a):
        return pltpu.VMEM(a.shape, a.dtype)

    def tile(*lead, dtype=F32):
        return pltpu.VMEM((*lead, ROWS, LANES), dtype)

    def wide(*lead, dtype):
        return pltpu.VMEM((*lead, ROWS, block), dtype)

    attended, layer_out = pl.pallas_call(
        kernel,
        out_shape=(
            jax.ShapeDtypeStruct((ROWS, HEADS * HEAD_DIM), BF16),
            jax.ShapeDtypeStruct((ROWS, width), BF16),
        ),
        in_specs=[smem, smem, vmem, hbm, vmem, hbm, vmem, hbm, hbm, hbm, vmem, hbm, hbm, hbm],
        out_specs=(vmem, vmem),
        scratch_shapes=[
            pltpu.VMEM((XS, vocab_rows, block), BF16),
            like(w_qkv), like(cache_keys), like(cache_values), like(w_out_t),
            like(w_gate), like(w_up), like(w_down),
            wide(XS, dtype=BF16), wide(XS - 1, dtype=BF16), tile(), tile(XS - 1),
            tile(PLANE), tile(PLANE - 1), tile(), tile(),
            tile(GROUPS, UNITS), tile(GROUPS, UNITS), tile(GROUPS, UNITS),
            tile(CHIPS - 1),
            pltpu.VMEM((ROWS, JOINT_HEADS * LANES), BF16),
            tile(GROUPS, per_group, 3), tile(GROUPS, per_group, 3), tile(GROUPS, per_group, 3),
            pltpu.VMEM((GROUPS, per_group, 2 * ROWS, LANES), BF16),
            pltpu.VMEM((CHIPS - 1, 2 * ROWS, LANES), BF16), tile(CHIPS + 1),
            pltpu.VMEM((ROWS, HEADS * LANES), BF16),
            tile(), tile(), tile(), tile(CHIPS, dtype=BF16),
            pltpu.VMEM((ROWS, model), BF16),
            wide(XS, dtype=BF16), wide(XS - 1, dtype=BF16), tile(PLANE), tile(PLANE - 1),
            tile(GROUP - 1, dtype=BF16),
            pltpu.SemaphoreType.DMA((XS,)),
            pltpu.SemaphoreType.DMA((7,)),
            pltpu.SemaphoreType.DMA((14,)),
            pltpu.SemaphoreType.DMA((14,)),
            pltpu.SemaphoreType.DMA((GROUPS,)),
            pltpu.SemaphoreType.DMA((KV_HEADS,)),
            pltpu.SemaphoreType.DMA((GROUPS,)),
        ],
        compiler_params=pltpu.CompilerParams(
            collective_id=0, has_side_effects=True, vmem_limit_bytes=60 * 2**20
        ),
        name="layer",
    )(
        token_ids.T, lengths, frequency, embed_table, attn_gain.reshape(-1, LANES), w_qkv,
        qkv_bias.reshape(-1, LANES), cache_keys, cache_values, w_out_t,
        mlp_gain.reshape(-1, LANES), w_gate, w_up, w_down,
    )
    return (
        attended.reshape(steps, prompts, -1),
        layer_out.reshape(steps, prompts, width),
    )


def solution(mesh):
    return jax.shard_map(
        body,
        mesh=mesh,
        in_specs=(
            P(None, "parts"), P("parts"), P("seq", None), P(), P("seq", None), P(),
            P("parts", "seq", None), P("parts", "seq", None), P(None, "seq"), P(),
            P(None, "seq"), P(None, "seq"), P("seq", None),
        ),
        out_specs=(P(None, "parts", None), P(None, "parts", "seq")),
        check_vma=False,
    )
```

time: 107 us -> 93.4 us (0.87)
  Pallas kernels: 103 us -> 89.8 us
    pallas_call x1, Pallas kernels: 103 us -> 89.8 us  [body(): pl.pallas_call(kernel, out_shape=(jax.ShapeDtypeStruct((ROWS, HEADS * HEA...]
where the time goes in v2:
time: 93.4 us; the launch traced here: 93.2 us
  Pallas kernels  89.8 us (96%)
  local copies, waits for them, and re-layouts  2.82 us (3%)
    pallas_call x1, Pallas kernels, body(): pl.pallas_call(kernel, out_shape=(jax.ShapeDtypeStruct((ROWS, HEADS * HEA...  89.8 us

profile of v2, /device:TPU:513, one launch (start us, length us, event | category | flops | bytes accessed | tf_op | source)
XLA Modules:
  0.0 93.2 jit_solution(15462952883105697738)
XLA Ops:
  0.6 89.8 %layer.1 = (bf16[8,5120]{1,0:T(8,128)(2,1)}, bf16[8,40]{1,0:T(8,128)(2,1)}) custom-call(s32[2,4]{1,0:T(2,128)} %bitcast.11, s32[2]{0:T(128)} %len_ref.1, f32[8,128]{1,0:T(8,128)} %constant.2.clone.freq_ref, bf16[594,5120]{1,0:T(8,128)(2,1)} %table_hbm.1, bf16[40,128]{1,0:T(8,128)(2,1)} %bitcast.8, bf16[40,7168]{1,0:T(8,128)(2,1)} %wqkv_hbm.1, ...), custom_call_target="tpu_custom_call" | custom-call | tf_op jit(solution)/shard_map/layer/pallas_call | solution.py:538
  90.4 1.6 %reshape.22 = bf16[4,2,5120]{2,1,0:T(2,128)(2,1)} reshape(bf16[8,5120]{1,0:T(8,128)(2,1)} %get-tuple-element.4) | data formatting | bytes 163840 | tf_op jit(solution)/shard_map/reshape | solution.py:581
  91.9 1.3 %copy.17 = bf16[4,2,40]{2,1,0:T(2,128)(2,1)} copy(bf16[4,2,40]{2,1,0:T(2,128)(2,1)} %bitcast.10) | data formatting | bytes 1280

commit v3 on v2

--- a/solution.py
+++ b/solution.py
@@ -121,12 +121,12 @@
     ids_ref, len_ref, freq_ref, table_hbm, gain_ref, wqkv_hbm, bias_ref, keys_hbm, values_hbm,
     wout_hbm, mgain_ref, wgate_hbm, wup_hbm, wdown_hbm,
     att_ref, lay_ref,
-    table, wqkv, keys, values, wout, wgate, wup, wdown,
+    table, wqkv, keys, values, wout, wgu, wdown,
     a1s, a1r, q1s, q1r, a2s, a2r, cosr, sinr,
-    po, bx, bs, br, jflat,
-    oo, ow, cx, cs, cr, levels, aflat, tmp, ds_, dx, mb, nflat,
+    bs, br, jflat,
+    cs, cr, levels, aflat, tmp, mb, nflat,
     es, er, e2s, e2r, dummy,
-    tsem, wsem, ssem, rsem, bxsem, jsem, cxsem,
+    tsem, wsem, ssem, rsem, jsem, osem, psem,
 ):
     me = lax.axis_index("seq")
     x = lax.div(me, PLANE)
@@ -159,26 +159,55 @@
                 send(tile, tile, send_sem, recv_sem, x_part[i] + y_part[j] + e)
         send(tile, tile, send_sem, recv_sem, other)
 
+    def to_core(tile, send_sem, recv_sem):
+        for i, j in chip_peers:
+            send(tile, tile, send_sem, recv_sem, x_part[i] + y_part[j] + c)
+
     barrier = pltpu.get_barrier_semaphore()
     for _, p in x_peers:
         pl.semaphore_signal(barrier, inc=1, device_id={"seq": p * PLANE + j0}, device_id_type=MESH)
+    order = [p for _, p in x_peers] + [x]
+    blocks = [pl.ds(pl.multiple_of(p * block, LANES), block) for p in order]
+    loads = []
+    for k, at in enumerate(blocks):
+        loads.append(pltpu.make_async_copy(table_hbm.at[:, at], table.at[k], tsem.at[k]))
+        loads[-1].start()
     for _, _, p in plane_peers:
         pl.semaphore_signal(barrier, inc=1, device_id={"seq": x * PLANE + p}, device_id_type=MESH)
-    order = [p for _, p in x_peers] + [x]
-    loads = []
-    for k, p in enumerate(order):
-        at = pl.ds(pl.multiple_of(p * block, LANES), block)
-        loads.append(pltpu.make_async_copy(table_hbm.at[:, at], table.at[k], tsem.at[k]))
-        loads[-1].start()
+
+    def parts(side):
+        def cols(start, n):
+            return pl.ds(pl.multiple_of(start * LANES, LANES), n * LANES)
+
+        out = []
+        for at, n, to in (
+            (HALF_HEADS * side, HALF_HEADS, 0),
+            (HEADS + GROUPS * side, GROUPS, HALF_HEADS),
+            (HEADS + KV_HEADS + GROUPS * side, GROUPS, HALF_HEADS + GROUPS),
+        ):
+            out.append((wqkv_hbm.at[:, cols(at, n)], wqkv.at[c, :, cols(to, n)]))
+        mine = cols(GROUPS * side, GROUPS)
+        out.append((keys_hbm.at[:, :, mine], keys.at[c]))
+        out.append((values_hbm.at[:, :, mine], values.at[c]))
+        out.append((wout_hbm, wout.at[c]))
+        return out
+
     weights = [
         pltpu.make_async_copy(src, dst, wsem.at[k])
         for k, (src, dst) in enumerate(
-            [(wqkv_hbm, wqkv), (keys_hbm, keys), (values_hbm, values), (wout_hbm, wout),
-             (wgate_hbm, wgate), (wup_hbm, wup), (wdown_hbm, wdown)]
+            parts(c) + [(wgate_hbm, wgu.at[:, :LANES]), (wup_hbm, wgu.at[:, LANES:])]
+            + [(wdown_hbm.at[:, at], wdown.at[k]) for k, at in enumerate(blocks)]
         )
     ]
     for w in weights:
         w.start()
+    swaps = [
+        pltpu.make_async_remote_copy(
+            src_ref=src, dst_ref=dst, send_sem=osem.at[k], recv_sem=psem.at[k],
+            device_id={"seq": other}, device_id_type=MESH,
+        )
+        for k, (src, dst) in enumerate(parts(1 - c))
+    ]
 
     lane = lax.broadcasted_iota(jnp.int32, (ROWS, LANES), 1)
     row = lax.broadcasted_iota(jnp.int32, (ROWS, LANES), 0)
@@ -209,6 +238,8 @@
     )
     for d, p in x_peers:
         send(q1s, q1r.at[d - 1], ssem.at[1], rsem.at[1], p * PLANE + j0)
+    for w in swaps:
+        w.start()
 
     place = jnp.zeros((ROWS, LANES), jnp.int32)
     for r in range(ROWS):
@@ -225,44 +256,43 @@
         total = total + a1r[k].astype(F32)
     found = [total[:, t * LANES : (t + 1) * LANES] for t in range(tiles)]
     square = q1s[...] + jnp.sum(q1r[...], axis=0)
-    for j, piece in enumerate(cut_pieces(found, width, PLANE)):
-        a2s[j] = jnp.where(low, piece, square)
+    pair = CORES * width
+    for j, piece in enumerate(cut_pieces(found, pair, YS)):
+        a2s[j] = jnp.where(lane < pair, piece, square)
     for k, e, p in plane_peers:
-        send(a2s.at[p], a2r.at[k * CORES + e - 1], ssem.at[2], rsem.at[2], x * PLANE + p)
-    weights[0].wait()
-    gain = own_gain(gain_ref[...].astype(F32), me, width)
+        to = lax.div(p, CORES)
+        send(a2s.at[to], a2r.at[k * CORES + e - 1], ssem.at[2], rsem.at[2], x * PLANE + p)
+    gain = own_gain(gain_ref[...].astype(F32), chip, pair)
+    for k in range(3):
+        weights[k].wait()
+        swaps[k].wait_recv()
     wait_bytes(a2r, rsem.at[2])
-    stream = a2s[j0] + jnp.sum(a2r[...], axis=0)
+    stream = a2s[y] + jnp.sum(a2r[...], axis=0)
     scale = lax.rsqrt(jnp.broadcast_to(stream[:, LANES - 1 :], (ROWS, LANES)) + NORM_EPS)
-    normed = (stream * scale * gain).astype(BF16)[:, :width]
+    normed = stream * scale * gain
+    normed = [
+        v[:, :width].astype(BF16) for v in (normed, pltpu.roll(normed, LANES - width, 1))
+    ]
 
     half_group = lax.div(chip, CHIPS // GROUPS)
     within = lax.rem(chip, CHIPS // GROUPS)
     far_groups = [lax.rem(half_group + k, GROUPS) for k in (2, 1, 3, 0)]
     near_groups = [lax.rem(half_group + k, GROUPS) for k in (0, 1, 3, 2)]
 
-    def project(side, g):
-        starts = [
-            (HALF_HEADS * side + group * g, group),
-            (HEADS + GROUPS * side + g, 1),
-            (HEADS + KV_HEADS + GROUPS * side + g, 1),
-        ]
-        out = []
-        for at, n in starts:
-            cols = pl.ds(pl.multiple_of(at * LANES, LANES), n * LANES)
-            got = jnp.dot(normed, wqkv[:, cols], preferred_element_type=F32)
-            out += [got[:, t * LANES : (t + 1) * LANES] for t in range(n)]
-        return out
+    def project(at, n):
+        cols = pl.ds(pl.multiple_of(at * LANES, LANES), n * LANES)
+        got = sum(
+            jnp.dot(normed[e], wqkv[e, :, cols], preferred_element_type=F32) for e in range(CORES)
+        )
+        return [got[:, t * LANES : (t + 1) * LANES] for t in range(n)]
 
     for n, g in enumerate(far_groups):
-        for r, v in enumerate(project(1 - c, g)):
-            po[n, r] = v
-        send(po.at[n], bx.at[n], ssem.at[4], bxsem.at[n], other)
-    for n, g in enumerate(far_groups):
-        mine = project(c, g)
-        wait_bytes(bx.at[n], bxsem.at[n])
+        mine = (
+            project(group * g, group) + project(HALF_HEADS + g, 1)
+            + project(HALF_HEADS + GROUPS + g, 1)
+        )
         for r in range(UNITS):
-            bs[n, r] = mine[r] + bx[n, r]
+            bs[n, r] = mine[r]
         for r in range(UNITS):
             p = (CHIPS // GROUPS) * g + JOINT_AT[r]
 
@@ -276,7 +306,7 @@
                 pl.when(within != JOINT_AT[r])(go)
 
     rb, b_on = position(within, JOINT_AT)
-    nb = UNITS * (GROUPS * c + half_group) + rb
+    nb = UNITS * half_group + rb
 
     @pl.when(b_on)
     def _():
@@ -294,66 +324,77 @@
         turn = jnp.where(rb <= group, 1.0, 0.0)
         jflat[:, lanes_of(nb)] = jnp.where(turn > 0.5, turned, joint).astype(BF16)
         tile = jflat.at[:, lanes_of(nb)]
-        to_all(tile, ssem.at[6], jsem.at[GROUPS * c + half_group])
-
-    weights[1].wait()
-    weights[2].wait()
-    span = keys.shape[1]
+        to_core(tile, ssem.at[6], jsem.at[half_group])
+
+    for k in range(3, 5):
+        weights[k].wait()
+        swaps[k].wait_recv()
+    span = keys.shape[2]
     lines = group * ROWS
-    wide_row = lax.broadcasted_iota(jnp.int32, (lines, span), 0)
+    wide_row = lax.broadcasted_iota(jnp.int32, (lines, CORES * span), 0)
     even = lax.rem(wide_row, prompts) == 0
-    where = me * span + lax.broadcasted_iota(jnp.int32, (lines, span), 1)
+    where = chip * (CORES * span) + lax.broadcasted_iota(jnp.int32, (lines, CORES * span), 1)
     valid = where < jnp.where(even, len_ref[0], len_ref[1])
     score_scale = 1.0 / math.sqrt(HEAD_DIM)
     nt = (((1,), (1,)), ((), ()))
 
-    def attend(side, g, into):
-        kv = GROUPS * side + g
-        base = UNITS * kv
-        at = lanes_of(kv)
+    def joint_group(g, n=UNITS):
+        return jflat.at[:, pl.ds(pl.multiple_of(g * UNITS * LANES, LANES), n * LANES)]
+
+    for n, g in enumerate(near_groups):
+        if n == 0:
+            @pl.when(b_on)
+            def _(g=g):
+                wait_bytes(joint_group(g, UNITS - 1), jsem.at[g])
+
+            @pl.when(jnp.logical_not(b_on))
+            def _(g=g):
+                wait_bytes(joint_group(g), jsem.at[g])
+        else:
+            wait_bytes(joint_group(g), jsem.at[g])
+        at = lanes_of(g)
         query = jnp.concatenate(
-            [jflat[:, lanes_of(base + r)].astype(F32) for r in range(group)], axis=0
+            [jflat[:, lanes_of(UNITS * g + r)].astype(F32) for r in range(group)], axis=0
         ).astype(BF16)
         score = [
-            lax.dot_general(query, keys[b, :, at], nt, preferred_element_type=F32)
+            jnp.concatenate(
+                [
+                    lax.dot_general(query, keys[e, b, :, at], nt, preferred_element_type=F32)
+                    for e in range(CORES)
+                ],
+                axis=1,
+            )
             for b in range(prompts)
         ]
         score = jnp.where(valid, jnp.where(even, score[0], score[1]) * score_scale, MASKED)
         top = jnp.max(score, axis=-1, keepdims=True)
         weight = jnp.where(valid, jnp.exp(score - top), 0.0)
         total = jnp.sum(weight, axis=-1, keepdims=True)
-        summed = jnp.dot(
-            jnp.where(even, weight, 0.0).astype(BF16), values[0, :, at], preferred_element_type=F32
-        ) + jnp.dot(
-            jnp.where(even, 0.0, weight).astype(BF16), values[1, :, at], preferred_element_type=F32
-        )
-        top = jnp.broadcast_to(top, (lines, LANES))
-        total = jnp.broadcast_to(total, (lines, LANES))
+        split = [
+            jnp.where(even, weight, 0.0).astype(BF16), jnp.where(even, 0.0, weight).astype(BF16)
+        ]
+        summed = sum(
+            jnp.dot(
+                split[b][:, e * span : (e + 1) * span], values[e, b, :, at],
+                preferred_element_type=F32,
+            )
+            for b in range(prompts)
+            for e in range(CORES)
+        )
+        some = total > 0.0
+        total = jnp.where(some, total, 1.0)
+        level = jnp.broadcast_to(
+            jnp.where(some, top + jnp.log(total), MASKED), (lines, LANES)
+        )
+        summed = summed / total
         for r in range(group):
-            into[r, 0] = summed[r * ROWS : (r + 1) * ROWS]
-            into[r, 1] = top[r * ROWS : (r + 1) * ROWS]
-            into[r, 2] = total[r * ROWS : (r + 1) * ROWS]
-
-    def joint_group(kv):
-        return jflat.at[:, pl.ds(pl.multiple_of(kv * UNITS * LANES, LANES), UNITS * LANES)]
-
-    def merge(n, g):
-        wait_bytes(cx.at[n], cxsem.at[n])
-        for r in range(group):
-            top_a, top_b = ow[n, r, 1], cx[n, r, 1]
-            top = jnp.maximum(top_a, top_b)
-            scale_a, scale_b = jnp.exp(top_a - top), jnp.exp(top_b - top)
-            summed = ow[n, r, 0] * scale_a + cx[n, r, 0] * scale_b
-            total = ow[n, r, 2] * scale_a + cx[n, r, 2] * scale_b
-            some = total > 0.0
-            total = jnp.where(some, total, 1.0)
-            level = jnp.where(some, top + jnp.log(total), MASKED)
-            cs[n, r] = packed(jnp.where(some, summed / total, 0.0), level)
+            own = slice(r * ROWS, (r + 1) * ROWS)
+            cs[n, r] = packed(summed[own], level[own])
         across = lax.rem(g + GROUPS // 2, GROUPS)
         for r in range(group):
             p = (CHIPS // GROUPS) * across + HEAD_AT[r]
 
-            def go(r=r, p=p):
+            def go(n=n, r=r, p=p):
                 slot = lax.rem(chip - p + CHIPS, CHIPS) - 1
                 send(cs.at[n, r], cr.at[slot], ssem.at[8], rsem.at[8], p * CORES + c)
 
@@ -362,35 +403,13 @@
             else:
                 pl.when(within != HEAD_AT[r])(go)
 
-    for n, g in enumerate(near_groups):
-        kv = GROUPS * (1 - c) + g
-        wait_bytes(joint_group(kv), jsem.at[kv])
-        attend(1 - c, g, oo.at[n])
-        send(oo.at[n], cx.at[n], ssem.at[7], cxsem.at[n], other)
-        kv = GROUPS * c + g
-        if n == 0:
-            @pl.when(b_on)
-            def _(kv=kv):
-                part = pl.ds(pl.multiple_of(kv * UNITS * LANES, LANES), (UNITS - 1) * LANES)
-                wait_bytes(jflat.at[:, part], jsem.at[kv])
-
-            @pl.when(jnp.logical_not(b_on))
-            def _(kv=kv):
-                wait_bytes(joint_group(kv), jsem.at[kv])
-        else:
-            wait_bytes(joint_group(kv), jsem.at[kv])
-        attend(c, g, ow.at[n])
-        if n:
-            merge(n - 1, near_groups[n - 1])
-    merge(GROUPS - 1, near_groups[-1])
-
     rc, c_on = position(within, HEAD_AT)
     gc = lax.rem(half_group + GROUPS // 2, GROUPS)
     hc = HALF_HEADS * c + group * gc + rc
 
     @pl.when(c_on)
     def _():
-        base = UNITS * (GROUPS * c + gc)
+        base = UNITS * gc
         query = jflat[:, lanes_of(base + rc)]
         new_key = jflat[:, lanes_of(base + group)]
         new_value = jflat[:, lanes_of(base + group + 1)]
@@ -433,25 +452,23 @@
     def _():
         wait_bytes(aflat, rsem.at[9])
 
-    weights[3].wait()
+    weights[5].wait()
+    swaps[5].wait_recv()
     attended = aflat[...]
     tmp[...] = jnp.zeros((ROWS, LANES), F32)
-    tmp[:, :width] = lax.dot_general(attended, wout[...], nt, preferred_element_type=F32)
-    mid = jnp.where(lane < width, tmp[...] + stream, 0.0)
-    mine = jnp.where(lax.rem(row * 0 + c, CORES) == 0, mid, pltpu.roll(mid, width, 1))
-    ds_[...] = mine
-    send(ds_, dx, ssem.at[10], rsem.at[10], other)
-    wait_bytes(dx, rsem.at[10])
-    mb[chip] = (mine + dx[...]).astype(BF16)
-    for i, j in chip_peers:
-        send(mb.at[chip], mb.at[chip], ssem.at[11], rsem.at[11], x_part[i] + y_part[j] + c)
+    for e in range(CORES):
+        tmp[:, e * width : (e + 1) * width] = lax.dot_general(
+            attended, wout[e], nt, preferred_element_type=F32
+        )
+    mid = jnp.where(lane < pair, tmp[...] + stream, 0.0)
+    mb[chip] = mid.astype(BF16)
+    to_core(mb.at[chip], ssem.at[11], rsem.at[11])
 
     att_ref[...] = attended
-    weights[4].wait()
-    weights[5].wait()
-    weights[6].wait()
+    for w in weights[6:]:
+        w.wait()
     wait_bytes(mb.at[pl.ds(0, CHIPS - 1)], rsem.at[11])
-    mids = join_pieces([mb[p].astype(F32) for p in range(CHIPS)], CORES * width, XS * tiles)
+    mids = join_pieces([mb[p].astype(F32) for p in range(CHIPS)], pair, XS * tiles)
     square = jnp.zeros((ROWS, LANES), F32)
     for v in mids:
         square = square + v * v
@@ -460,12 +477,11 @@
     for g, v in enumerate(mids):
         nflat[:, g * LANES : (g + 1) * LANES] = (v * scale * gain[g : g + 1, :]).astype(BF16)
     normed_mid = nflat[...]
-    gate = jnp.dot(normed_mid, wgate[...], preferred_element_type=F32)
-    upper = jnp.dot(normed_mid, wup[...], preferred_element_type=F32)
+    both = jnp.dot(normed_mid, wgu[...], preferred_element_type=F32)
+    gate, upper = both[:, :LANES], both[:, LANES:]
     hidden = (gate / (1.0 + jnp.exp(-gate)) * upper).astype(BF16)
     for k, p in enumerate(order):
-        at = pl.ds(pl.multiple_of(p * block, LANES), block)
-        es[k] = jnp.dot(hidden, wdown[:, at], preferred_element_type=F32).astype(BF16)
+        es[k] = jnp.dot(hidden, wdown[k], preferred_element_type=F32).astype(BF16)
         if k < XS - 1:
             d = x_peers[k][0]
             send(es.at[k], er.at[d - 1], ssem.at[12], rsem.at[12], p * PLANE + j0)
@@ -475,23 +491,28 @@
         total = total + er[k].astype(F32)
     found = [total[:, t * LANES : (t + 1) * LANES] for t in range(tiles)]
     for j, piece in enumerate(cut_pieces(found, width, PLANE)):
-        e2s[j] = piece
+        e2s[j] = piece.astype(BF16)
     for k, e, p in plane_peers:
         send(e2s.at[p], e2r.at[k * CORES + e - 1], ssem.at[13], rsem.at[13], x * PLANE + p)
     wait_bytes(e2r, rsem.at[13])
-    final = mid + e2s[j0] + jnp.sum(e2r[...], axis=0)
+    final = e2s[j0].astype(F32)
+    for k in range(PLANE - 1):
+        final = final + e2r[k].astype(F32)
+    final = final + jnp.where(row * 0 + c == 0, mid, pltpu.roll(mid, LANES - width, 1))
     lay_ref[...] = final[:, :width].astype(BF16)
 
     for sem, ref in (
-        (0, a1r), (1, q1r), (2, a2r), (4, bx), (7, cx), (10, dx), (12, er), (13, e2r),
+        (0, a1r), (1, q1r), (2, a2r), (12, er), (13, e2r),
     ):
         wait_bytes(ref, ssem.at[sem])
     wait_bytes(mb.at[pl.ds(0, CHIPS - 1)], ssem.at[11])
+    for w in swaps:
+        w.wait_send()
 
     @pl.when(b_on)
     def _():
         wait_bytes(br.at[pl.ds(0, HALF_JOINT - 1)], ssem.at[5])
-        wait_bytes(dummy, ssem.at[6])
+        wait_bytes(mb.at[pl.ds(0, CHIPS - 1)], ssem.at[6])
 
     @pl.when(jnp.logical_not(b_on))
     def _():
@@ -513,6 +534,7 @@
 ):
     steps, prompts = token_ids.shape
     vocab_rows, model = embed_table.shape
+    span = cache_keys.shape[1]
     width = w_out.shape[1]
     block = PLANE * width
     per_group = HEADS // KV_HEADS
@@ -545,28 +567,30 @@
         out_specs=(vmem, vmem),
         scratch_shapes=[
             pltpu.VMEM((XS, vocab_rows, block), BF16),
-            like(w_qkv), like(cache_keys), like(cache_values), like(w_out_t),
-            like(w_gate), like(w_up), like(w_down),
+            pltpu.VMEM((CORES, width, HALF_JOINT * LANES), BF16),
+            pltpu.VMEM((CORES, prompts, span, GROUPS * LANES), BF16),
+            pltpu.VMEM((CORES, prompts, span, GROUPS * LANES), BF16),
+            pltpu.VMEM((CORES, width, model), BF16),
+            pltpu.VMEM((model, 2 * LANES), BF16), pltpu.VMEM((XS, LANES, block), BF16),
             wide(XS, dtype=BF16), wide(XS - 1, dtype=BF16), tile(), tile(XS - 1),
-            tile(PLANE), tile(PLANE - 1), tile(), tile(),
-            tile(GROUPS, UNITS), tile(GROUPS, UNITS), tile(GROUPS, UNITS),
-            tile(CHIPS - 1),
-            pltpu.VMEM((ROWS, JOINT_HEADS * LANES), BF16),
-            tile(GROUPS, per_group, 3), tile(GROUPS, per_group, 3), tile(GROUPS, per_group, 3),
+            tile(YS), tile(PLANE - 1), tile(), tile(),
+            tile(GROUPS, UNITS), tile(CHIPS - 1),
+            pltpu.VMEM((ROWS, HALF_JOINT * LANES), BF16),
             pltpu.VMEM((GROUPS, per_group, 2 * ROWS, LANES), BF16),
             pltpu.VMEM((CHIPS - 1, 2 * ROWS, LANES), BF16), tile(CHIPS + 1),
             pltpu.VMEM((ROWS, HEADS * LANES), BF16),
-            tile(), tile(), tile(), tile(CHIPS, dtype=BF16),
+            tile(), tile(CHIPS, dtype=BF16),
             pltpu.VMEM((ROWS, model), BF16),
-            wide(XS, dtype=BF16), wide(XS - 1, dtype=BF16), tile(PLANE), tile(PLANE - 1),
+            wide(XS, dtype=BF16), wide(XS - 1, dtype=BF16),
+            tile(PLANE, dtype=BF16), tile(PLANE - 1, dtype=BF16),
             tile(GROUP - 1, dtype=BF16),
             pltpu.SemaphoreType.DMA((XS,)),
-            pltpu.SemaphoreType.DMA((7,)),
+            pltpu.SemaphoreType.DMA((8 + XS,)),
             pltpu.SemaphoreType.DMA((14,)),
             pltpu.SemaphoreType.DMA((14,)),
             pltpu.SemaphoreType.DMA((GROUPS,)),
-            pltpu.SemaphoreType.DMA((KV_HEADS,)),
-            pltpu.SemaphoreType.DMA((GROUPS,)),
+            pltpu.SemaphoreType.DMA((6,)),
+            pltpu.SemaphoreType.DMA((6,)),
         ],
         compiler_params=pltpu.CompilerParams(
             collective_id=0, has_side_effects=True, vmem_limit_bytes=60 * 2**20

time: 93.4 us -> 87.4 us (0.936)
  Pallas kernels: 89.8 us -> 83.7 us
    pallas_call x1, Pallas kernels: 89.8 us -> 83.7 us  [body(): pl.pallas_call(kernel, out_shape=(jax.ShapeDtypeStruct((ROWS, HEADS * HEA...]
where the time goes in v3:
time: 87.4 us; the launch traced here: 87.2 us
  Pallas kernels  83.7 us (96%)
  local copies, waits for them, and re-layouts  2.82 us (3%)
    pallas_call x1, Pallas kernels, body(): pl.pallas_call(kernel, out_shape=(jax.ShapeDtypeStruct((ROWS, HEADS * HEA...  83.7 us

profile of v3, /device:TPU:513, one launch (start us, length us, event | category | flops | bytes accessed | tf_op | source)
XLA Modules:
  0.0 87.2 jit_solution(8082414595010859284)
XLA Ops:
  0.6 83.7 %layer.1 = (bf16[8,5120]{1,0:T(8,128)(2,1)}, bf16[8,40]{1,0:T(8,128)(2,1)}) custom-call(s32[2,4]{1,0:T(2,128)} %bitcast.11, s32[2]{0:T(128)} %len_ref.1, f32[8,128]{1,0:T(8,128)} %constant.2.clone.freq_ref, bf16[594,5120]{1,0:T(8,128)(2,1)} %table_hbm.1, bf16[40,128]{1,0:T(8,128)(2,1)} %bitcast.8, bf16[40,7168]{1,0:T(8,128)(2,1)} %wqkv_hbm.1, ...), custom_call_target="tpu_custom_call" | custom-call | tf_op jit(solution)/shard_map/layer/pallas_call | solution.py:560
  84.4 1.6 %reshape.22 = bf16[4,2,5120]{2,1,0:T(2,128)(2,1)} reshape(bf16[8,5120]{1,0:T(8,128)(2,1)} %get-tuple-element.4) | data formatting | bytes 163840 | tf_op jit(solution)/shard_map/reshape | solution.py:605
  85.9 1.3 %copy.17 = bf16[4,2,40]{2,1,0:T(2,128)(2,1)} copy(bf16[4,2,40]{2,1,0:T(2,128)(2,1)} %bitcast.10) | data formatting | bytes 1280

commit v4 on v3

--- a/solution.py
+++ b/solution.py
@@ -69,17 +69,25 @@
     copy.start()
 
 
-def packed(value, level):
-    lane = lax.broadcasted_iota(jnp.int32, (ROWS, LANES), 1)
+def split_level(level):
+    lane = lax.broadcasted_iota(jnp.int32, level.shape, 1)
     first = level.astype(BF16).astype(F32)
     second = (level - first).astype(BF16).astype(F32)
     third = level - first - second
     quarter = LANES // 4
-    parts = jnp.where(
+    return jnp.where(
         lane < quarter, first,
         jnp.where(lane < 2 * quarter, second, jnp.where(lane < 3 * quarter, third, 0.0)),
     )
-    return jnp.concatenate([value, parts], axis=0).astype(BF16)
+
+
+def join_level(parts):
+    level = parts + pltpu.roll(parts, LANES // 2, 1)
+    return level + pltpu.roll(level, LANES // 4, 1)
+
+
+def packed(value, level):
+    return jnp.concatenate([value, split_level(level)], axis=0).astype(BF16)
 
 
 def wait_bytes(ref, sem):
@@ -122,7 +130,7 @@
     wout_hbm, mgain_ref, wgate_hbm, wup_hbm, wdown_hbm,
     att_ref, lay_ref,
     table, wqkv, keys, values, wout, wgu, wdown,
-    a1s, a1r, q1s, q1r, a2s, a2r, cosr, sinr,
+    a1s, a1r, a2s, a2r, cosr, sinr,
     bs, br, jflat,
     cs, cr, levels, aflat, tmp, mb, nflat,
     es, er, e2s, e2r, dummy,
@@ -224,20 +232,18 @@
     for k in range(XS):
         loads[k].wait()
         found = jnp.dot(chosen, table[k], preferred_element_type=F32)
-        a1s[k] = found.astype(BF16)
+        a1s[k, :, :block] = found.astype(BF16)
         for t in range(tiles):
             v = found[:, t * LANES : (t + 1) * LANES]
             square = square + v * v
-        if k == 0:
-            pl.semaphore_wait(barrier, XS + PLANE - 2)
-        if k < XS - 1:
-            d, p = x_peers[k]
-            send(a1s.at[k], a1r.at[d - 1], ssem.at[0], rsem.at[0], p * PLANE + j0)
-    q1s[...] = jnp.broadcast_to(
-        jnp.sum(square, axis=-1, keepdims=True) / (XS * block), (ROWS, LANES)
-    )
-    for d, p in x_peers:
-        send(q1s, q1r.at[d - 1], ssem.at[1], rsem.at[1], p * PLANE + j0)
+    square = split_level(
+        jnp.broadcast_to(jnp.sum(square, axis=-1, keepdims=True) / (XS * block), (ROWS, LANES))
+    ).astype(BF16)
+    for k in range(XS):
+        a1s[k, :, block:] = square
+    pl.semaphore_wait(barrier, XS + PLANE - 2)
+    for k, (d, p) in enumerate(x_peers):
+        send(a1s.at[k], a1r.at[d - 1], ssem.at[0], rsem.at[0], p * PLANE + j0)
     for w in swaps:
         w.start()
 
@@ -250,12 +256,11 @@
     sinr[...] = jnp.where(lane < HEAD_DIM // 2, -sine, sine)
 
     wait_bytes(a1r, rsem.at[0])
-    wait_bytes(q1r, rsem.at[1])
     total = a1s[XS - 1].astype(F32)
     for k in range(XS - 1):
         total = total + a1r[k].astype(F32)
     found = [total[:, t * LANES : (t + 1) * LANES] for t in range(tiles)]
-    square = q1s[...] + jnp.sum(q1r[...], axis=0)
+    square = join_level(total[:, block:])
     pair = CORES * width
     for j, piece in enumerate(cut_pieces(found, pair, YS)):
         a2s[j] = jnp.where(lane < pair, piece, square)
@@ -433,9 +438,7 @@
             return cs[GROUPS - 1, rc] if s == CHIPS - 1 else cr[s]
 
         for s in range(CHIPS):
-            level = partial(s)[ROWS:].astype(F32)
-            level = level + pltpu.roll(level, LANES // 2, 1)
-            level = level + pltpu.roll(level, LANES // 4, 1)
+            level = join_level(partial(s)[ROWS:].astype(F32))
             levels[s] = level
             best = jnp.maximum(best, level)
         den = jnp.exp(levels[CHIPS] - best)
@@ -480,11 +483,13 @@
     both = jnp.dot(normed_mid, wgu[...], preferred_element_type=F32)
     gate, upper = both[:, :LANES], both[:, LANES:]
     hidden = (gate / (1.0 + jnp.exp(-gate)) * upper).astype(BF16)
-    for k, p in enumerate(order):
-        es[k] = jnp.dot(hidden, wdown[k], preferred_element_type=F32).astype(BF16)
-        if k < XS - 1:
-            d = x_peers[k][0]
-            send(es.at[k], er.at[d - 1], ssem.at[12], rsem.at[12], p * PLANE + j0)
+    for batch in (range(XS // 2), range(XS // 2, XS)):
+        for k in batch:
+            es[k] = jnp.dot(hidden, wdown[k], preferred_element_type=F32).astype(BF16)
+        for k in batch:
+            if k < XS - 1:
+                d, p = x_peers[k]
+                send(es.at[k], er.at[d - 1], ssem.at[12], rsem.at[12], p * PLANE + j0)
     wait_bytes(er, rsem.at[12])
     total = es[XS - 1].astype(F32)
     for k in range(XS - 1):
@@ -502,7 +507,7 @@
     lay_ref[...] = final[:, :width].astype(BF16)
 
     for sem, ref in (
-        (0, a1r), (1, q1r), (2, a2r), (12, er), (13, e2r),
+        (0, a1r), (2, a2r), (12, er), (13, e2r),
     ):
         wait_bytes(ref, ssem.at[sem])
     wait_bytes(mb.at[pl.ds(0, CHIPS - 1)], ssem.at[11])
@@ -557,11 +562,14 @@
     def wide(*lead, dtype):
         return pltpu.VMEM((*lead, ROWS, block), dtype)
 
+    def wider(*lead):
+        return pltpu.VMEM((*lead, ROWS, block + LANES), BF16)
+
     attended, layer_out = pl.pallas_call(
         kernel,
         out_shape=(
-            jax.ShapeDtypeStruct((ROWS, HEADS * HEAD_DIM), BF16),
-            jax.ShapeDtypeStruct((ROWS, width), BF16),
+            pltpu.VMEM((ROWS, HEADS * HEAD_DIM), BF16),
+            pltpu.VMEM((ROWS, width), BF16),
         ),
         in_specs=[smem, smem, vmem, hbm, vmem, hbm, vmem, hbm, hbm, hbm, vmem, hbm, hbm, hbm],
         out_specs=(vmem, vmem),
@@ -572,7 +580,7 @@
             pltpu.VMEM((CORES, prompts, span, GROUPS * LANES), BF16),
             pltpu.VMEM((CORES, width, model), BF16),
             pltpu.VMEM((model, 2 * LANES), BF16), pltpu.VMEM((XS, LANES, block), BF16),
-            wide(XS, dtype=BF16), wide(XS - 1, dtype=BF16), tile(), tile(XS - 1),
+            wider(XS), wider(XS - 1),
             tile(YS), tile(PLANE - 1), tile(), tile(),
             tile(GROUPS, UNITS), tile(CHIPS - 1),
             pltpu.VMEM((ROWS, HALF_JOINT * LANES), BF16),
@@ -601,10 +609,26 @@
         qkv_bias.reshape(-1, LANES), cache_keys, cache_values, w_out_t,
         mlp_gain.reshape(-1, LANES), w_gate, w_up, w_down,
     )
-    return (
-        attended.reshape(steps, prompts, -1),
-        layer_out.reshape(steps, prompts, width),
+    return pl.pallas_call(
+        finish,
+        out_shape=(
+            jax.ShapeDtypeStruct((steps, prompts, HEADS * HEAD_DIM), BF16),
+            jax.ShapeDtypeStruct((steps, prompts, width), BF16),
+        ),
+        in_specs=[vmem, vmem],
+        out_specs=(vmem, vmem),
+        name="finish",
+    )(
+        pltpu.with_memory_space_constraint(attended, pltpu.VMEM),
+        pltpu.with_memory_space_constraint(layer_out, pltpu.VMEM),
     )
+
+
+def finish(att_ref, lay_ref, att_out, lay_out):
+    n = att_out.shape[1]
+    for k in range(att_out.shape[0]):
+        att_out[k] = att_ref[k * n : (k + 1) * n]
+        lay_out[k] = lay_ref[k * n : (k + 1) * n]
 
 
 def solution(mesh):

time: 87.4 us -> 82.6 us (0.945)
  local copies, waits for them, and re-layouts: 2.82 us -> 0 us
  Pallas kernels: 83.7 us -> 81.7 us
    pallas_call x1 -> x2, Pallas kernels: 83.7 us -> 81.7 us  [the longest x1 81.1 us: body(): pl.pallas_call(kernel, out_shape=(pltpu.VMEM((ROWS, HEADS * HEAD_DIM), BF...]
    reshape x1 -> x0, local copies, waits for them, and re-layouts: 1.56 us -> none  [body(): attended.reshape(steps, prompts, -1)]
    unnamed x1 -> x0, local copies, waits for them, and re-layouts: 1.26 us -> none
where the time goes in v4:
time: 82.6 us; the launch traced here: 82.4 us
  Pallas kernels  81.7 us (99%)
    pallas_call x1, Pallas kernels, body(): pl.pallas_call(kernel, out_shape=(pltpu.VMEM((ROWS, HEADS * HEAD_DIM), BF...  81.1 us

profile of v4, /device:TPU:513, one launch (start us, length us, event | category | flops | bytes accessed | tf_op | source)
XLA Modules:
  0.0 82.4 jit_solution(9055175833582645492)
XLA Ops:
  0.6 81.1 %layer.1 = (bf16[8,5120]{1,0:T(8,128)(2,1)S(1)}, bf16[8,40]{1,0:T(8,128)(2,1)S(1)}) custom-call(s32[2,4]{1,0:T(2,128)} %bitcast.9, s32[2]{0:T(128)} %len_ref.1, f32[8,128]{1,0:T(8,128)} %constant.2.clone.freq_ref, bf16[594,5120]{1,0:T(8,128)(2,1)} %table_hbm.1, bf16[40,128]{1,0:T(8,128)(2,1)} %bitcast.7, bf16[40,7168]{1,0:T(8,128)(2,1)} %wqkv_hbm.1, ...), custom_call_target="tpu_custom_call" | custom-call | tf_op jit(solution)/shard_map/layer/pallas_call | solution.py:568
  81.7 0.7 finish.1

commit v5 on v4

--- a/solution.py
+++ b/solution.py
@@ -483,7 +483,7 @@
     both = jnp.dot(normed_mid, wgu[...], preferred_element_type=F32)
     gate, upper = both[:, :LANES], both[:, LANES:]
     hidden = (gate / (1.0 + jnp.exp(-gate)) * upper).astype(BF16)
-    for batch in (range(XS // 2), range(XS // 2, XS)):
+    for batch in (range(2), range(2, XS)):
         for k in batch:
             es[k] = jnp.dot(hidden, wdown[k], preferred_element_type=F32).astype(BF16)
         for k in batch:

time: 82.6 us -> 82.6 us (level)
  no operation moved by 1% of the time
where the time goes in v5:
time: 82.6 us; the launch traced here: 82.4 us
  Pallas kernels  81.8 us (99%)
    pallas_call x1, Pallas kernels, body(): pl.pallas_call(kernel, out_shape=(pltpu.VMEM((ROWS, HEADS * HEAD_DIM), BF...  81.1 us

profile of v5, /device:TPU:513, one launch (start us, length us, event | category | flops | bytes accessed | tf_op | source)
XLA Modules:
  0.0 82.4 jit_solution(2007291341804973217)
XLA Ops:
  0.6 81.1 %layer.1 = (bf16[8,5120]{1,0:T(8,128)(2,1)S(1)}, bf16[8,40]{1,0:T(8,128)(2,1)S(1)}) custom-call(s32[2,4]{1,0:T(2,128)} %bitcast.9, s32[2]{0:T(128)} %len_ref.1, f32[8,128]{1,0:T(8,128)} %constant.2.clone.freq_ref, bf16[594,5120]{1,0:T(8,128)(2,1)} %table_hbm.1, bf16[40,128]{1,0:T(8,128)(2,1)} %bitcast.7, bf16[40,7168]{1,0:T(8,128)(2,1)} %wqkv_hbm.1, ...), custom_call_target="tpu_custom_call" | custom-call | tf_op jit(solution)/shard_map/layer/pallas_call | solution.py:568
  81.8 0.7 finish.1
